TPU v7x, 32 devices: a 4x4x1 block of a 4x4x8 slice. The times are simulated.
32 devices in a mesh: inst: 1 (over z), dev: 4 (over y), side: 8 (over x, core).
Axes of the slice: x: 4, y: 4, z: 1, core: 2. Of those that a mesh axis runs over, the one named last changes fastest.
The devices are a block of a 4x4x8 slice.
Arguments:
- hidden: bfloat16 [512, 3584], P(('inst', 'dev'))
- cache_len: int32 [512], P(('inst', 'dev'))
- k_cache: bfloat16 [1, 512, 8, 64, 256], P(None, ('inst', 'dev'))
- v_cache: bfloat16 [1, 512, 8, 64, 256], P(None, ('inst', 'dev'))
- w_q: bfloat16 [1, 3584, 4096], replicated
- w_kv: bfloat16 [1, 3584, 4096], replicated
- w_o: bfloat16 [1, 4096, 3584], replicated
- attn_gain: float32 [1, 3584], replicated
- ffn_gain: float32 [1, 3584], replicated
- w_gate: bfloat16 [1, 3584, 14336], P(None, None, 'dev')
- w_up: bfloat16 [1, 3584, 14336], P(None, None, 'dev')
- w_down: bfloat16 [1, 14336, 3584], P(None, 'dev')
Outputs:
- output: bfloat16 [512, 3584], P(('inst', 'dev', 'side'))
All inputs are finite; a program needn't handle non-finite values.
Results may differ from a plain program's by a relative error of at most 0.0123053.
Values are sent between devices in bfloat16 or wider.
A program may use at most 768 MiB of HBM per device.

v0:
```python
import jax
import jax.numpy as jnp
from jax import lax
from jax.sharding import PartitionSpec as P

EPS = 1e-5
ROPE_BASE = 10000.0


def rms_norm(rows, gain):
    rows_f = rows.astype(jnp.float32)
    inv_rms = lax.rsqrt(jnp.mean(rows_f * rows_f, axis=-1, keepdims=True) + EPS)
    return (rows_f * inv_rms * gain).astype(jnp.bfloat16)


def rotary(vecs, positions):
    half_dim = vecs.shape[-1] // 2
    freqs = ROPE_BASE ** (-jnp.arange(half_dim, dtype=jnp.float32) / half_dim)
    angle = positions.astype(jnp.float32)[:, None, None] * freqs
    cos_part = jnp.cos(angle)
    sin_part = jnp.sin(angle)
    first = vecs[..., :half_dim]
    second = vecs[..., half_dim:]
    return jnp.concatenate([first * cos_part - second * sin_part, second * cos_part + first * sin_part], axis=-1)


def attention_layer(x_rows, lengths, k_seq, v_seq, q_weight, kv_weight, o_weight, gain_attn):
    count = x_rows.shape[0]
    kv_heads = k_seq.shape[1]
    head_dim = k_seq.shape[-1]
    normed = rms_norm(x_rows, gain_attn)
    q_all = jnp.dot(normed, q_weight, preferred_element_type=jnp.float32).reshape(count, -1, head_dim)
    kv_all = jnp.dot(normed, kv_weight, preferred_element_type=jnp.float32).reshape(count, 2, kv_heads, head_dim)
    q_rows = rotary(q_all, lengths).astype(jnp.bfloat16).reshape(count, kv_heads, -1, head_dim)
    k_new = rotary(kv_all[:, 0], lengths).astype(jnp.bfloat16)
    v_new = kv_all[:, 1].astype(jnp.bfloat16)
    scale = head_dim ** -0.5
    scores = jnp.einsum('nkgd,nksd->nkgs', q_rows, k_seq, preferred_element_type=jnp.float32) * scale
    valid = jnp.arange(k_seq.shape[2])[None, None, None, :] < lengths[:, None, None, None]
    scores = jnp.where(valid, scores, -1e30)
    self_score = jnp.einsum('nkgd,nkd->nkg', q_rows, k_new, preferred_element_type=jnp.float32) * scale
    row_max = jnp.maximum(jnp.max(scores, axis=-1), self_score)
    exp_scores = jnp.exp(scores - row_max[..., None])
    self_exp = jnp.exp(self_score - row_max)
    total_exp = jnp.sum(exp_scores, axis=-1) + self_exp
    mixed = jnp.einsum('nkgs,nksd->nkgd', exp_scores.astype(jnp.bfloat16), v_seq, preferred_element_type=jnp.float32)
    mixed = mixed + self_exp.astype(jnp.bfloat16).astype(jnp.float32)[..., None] * v_new.astype(jnp.float32)[:, :, None, :]
    mixed = (mixed / total_exp[..., None]).astype(jnp.bfloat16).reshape(count, -1)
    attn_out = jnp.dot(mixed, o_weight, preferred_element_type=jnp.float32)
    return (x_rows.astype(jnp.float32) + attn_out).astype(jnp.bfloat16)


def ffn_partial(h_rows, gate_weight, up_weight, down_weight):
    gate = jnp.dot(h_rows, gate_weight, preferred_element_type=jnp.float32)
    up_proj = jnp.dot(h_rows, up_weight, preferred_element_type=jnp.float32)
    act_rows = (jax.nn.silu(gate) * up_proj).astype(jnp.bfloat16)
    return jnp.dot(act_rows, down_weight, preferred_element_type=jnp.float32)


def pair_rows(local, slot, half_side):
    shaped = local.reshape((2, half_side, local.shape[0] // (2 * half_side)) + local.shape[1:])
    picked = lax.dynamic_index_in_dim(shaped, slot, axis=1, keepdims=False)
    return picked.reshape((-1,) + local.shape[1:])


def keep_rows(x_in):
    return x_in


def skip_ffn(h_in):
    return jnp.zeros(h_in.shape, jnp.float32)


def solution(mesh):
    n_side = mesh.shape['side']
    half_side = n_side // 2
    to_ffn = [(slot, slot + half_side) for slot in range(half_side)]
    to_attn = [(slot + half_side, slot) for slot in range(half_side)]
    batch_axes = ('inst', 'dev')
    in_specs = (
        P(batch_axes, None),
        P(batch_axes),
        P(None, batch_axes, None, None, None),
        P(None, batch_axes, None, None, None),
        P(), P(), P(), P(), P(),
        P(None, None, 'dev'),
        P(None, None, 'dev'),
        P(None, 'dev', None),
    )
    out_specs = P(('inst', 'dev', 'side'), None)

    def device_fn(hidden, cache_len, k_cache, v_cache, w_q, w_kv, w_o, attn_gain, ffn_gain, w_gate, w_up, w_down):
        side_idx = lax.axis_index('side')
        is_attn = side_idx < half_side
        slot = side_idx % half_side
        rows = hidden.shape[0] // n_side
        n_layers = w_q.shape[0]
        x_pair = pair_rows(hidden, slot, half_side)
        lengths = pair_rows(cache_len, slot, half_side)
        for layer in range(n_layers):
            def attn_branch(x_in, layer=layer):
                k_seq = pair_rows(k_cache[layer], slot, half_side)
                v_seq = pair_rows(v_cache[layer], slot, half_side)
                return attention_layer(x_in, lengths, k_seq, v_seq, w_q[layer], w_kv[layer], w_o[layer], attn_gain[layer])

            def ffn_branch(h_in, layer=layer):
                return ffn_partial(h_in, w_gate[layer], w_up[layer], w_down[layer])

            x_pair = lax.cond(is_attn, attn_branch, keep_rows, x_pair)
            sent = lax.ppermute(x_pair, 'side', to_ffn)
            h_rows = rms_norm(sent, ffn_gain[layer])
            h_all = lax.all_gather(h_rows, 'dev', axis=0, tiled=True)
            part_sum = lax.cond(is_attn, skip_ffn, ffn_branch, h_all)
            summed = lax.psum_scatter(part_sum, 'dev', scatter_dimension=0, tiled=True)
            x_ffn = (sent.astype(jnp.float32) + summed.astype(jnp.bfloat16).astype(jnp.float32)).astype(jnp.bfloat16)
            if layer + 1 < n_layers:
                x_pair = lax.ppermute(x_ffn, 'side', to_attn)
            else:
                back = lax.ppermute(x_ffn[:rows], 'side', to_attn)
                out_rows = jnp.where(is_attn, back, x_ffn[rows:])
        return out_rows

    return jax.shard_map(device_fn, mesh=mesh, in_specs=in_specs, out_specs=out_specs, check_vma=False)
```

profile of v0, /device:TPU:97, one launch (start us, length us, event | category | flops | bytes accessed | tf_op | source)
XLA Modules:
  0.0 245.2 jit_solution(880897713757159522)
XLA Ops:
  6.5 0.0 copy-start
  6.6 0.0 reduce-scatter.2.cloned.1.call-start
  6.6 1.2 copy-done
  7.7 0.0 copy-start.2
  7.8 137.7 %conditional.2 = (bf16[32,3584]{1,0:T(8,128)(2,1)S(1)}) conditional(s32[]{:T(128)} %convert_element_type.68, bf16[32,3584]{1,0:T(8,128)(2,1)S(1)} %bitcast.102, (bf16[32,3584]{1,0:T(8,128)(2,1)S(1)}, s32[128]{0:T(128)}, f32[1,3584]{1,0:T(1,128)}, bf16[1,3584,4096]{2,1,0:T(8,128)(2,1)}, bf16[1,128,8,64,256]{4,3,2,1,0:T(8,128)(2,1)}, ...), branch_computations={%region_0.1_spmd, %region_1.5_spmd.clone} | conditional | flops 2855872000 | bytes 264011744 | solution.py:109
  7.8 0.2 fusion.32
  8.0 0.8 reduce
  8.7 36.0 %copy.41 = bf16[1,3584,4096]{1,2,0:T(8,128)(2,1)} copy(bf16[1,3584,4096]{2,1,0:T(8,128)(2,1)} %get-tuple-element.93) | data formatting | bytes 58720256 | tf_op jit(solution)/shard_map
  44.7 0.0 copy-start.3
  44.7 13.9 %fusion.37 = f32[32,2,8,256]{3,0,2,1:T(8,128)S(1)} fusion(bf16[2,8,256,3584]{3,2,1,0:T(8,128)(2,1)} %bitcast.99, bf16[32,3584]{1,0:T(8,128)(2,1)S(1)} %get-tuple-element.88, f32[3584]{0:T(1024)S(1)} %reduce, f32[32]{0:T(128)S(1)} %add_rsqrt_fusion), kind=kOutput, calls=%fused_computation.36 | convolution fusion | flops 939982848 | bytes 30128256 | tf_op jit(solution)/shard_map/cond/branch_1_fun/dot_general | solution.py:33
  58.6 0.0 copy-done.3
  58.6 0.1 reshape.164
  58.7 0.1 reshape.163
  58.8 0.1 multiply_cosine_fusion
  59.1 36.0 %copy.40 = bf16[1,3584,4096]{1,2,0:T(8,128)(2,1)} copy(bf16[1,3584,4096]{2,1,0:T(8,128)(2,1)} %get-tuple-element.90) | data formatting | bytes 58720256 | tf_op jit(solution)/shard_map
  95.1 13.9 %fusion.39 = f32[32,16,256]{2,0,1:T(8,128)S(1)} fusion(bf16[16,256,3584]{2,1,0:T(8,128)(2,1)} %bitcast.98, bf16[32,3584]{1,0:T(8,128)(2,1)S(1)} %get-tuple-element.88, f32[3584]{0:T(1024)S(1)} %reduce, f32[32]{0:T(128)S(1)} %add_rsqrt_fusion), kind=kOutput, calls=%fused_computation.38 | convolution fusion | flops 939982848 | bytes 30128256 | tf_op jit(solution)/shard_map/cond/branch_1_fun/dot_general | solution.py:32
  108.9 0.1 add_convert_fusion
  109.0 0.1 copy_dynamic-update-slice_fusion.1
  109.1 0.2 copy_dynamic-update-slice_fusion
  109.3 0.4 fusion.35
  109.8 11.8 %constant_dynamic-slice_fusion.1 = (bf16[2,1,16,8,64,256]{5,4,3,2,1,0:T(8,128)(2,1)}, bf16[2,1,16,8,64,256]{5,4,3,2,1,0:T(8,128)(2,1)}) fusion(bf16[2,4,16,8,64,256]{5,4,3,2,1,0:T(8,128)(2,1)} %bitcast.105, s32[]{:T(128)S(6)} %select_n.34, bf16[2,4,16,8,64,256]{5,4,3,2,1,0:T(8,128)(2,1)} %bitcast.104), kind=kLoop, calls=%fused_computation.58 | loop fusion | bytes 33554436 | tf_op jit(solution)/shard_map/cond/branch_1_fun/jit(dynamic_index_in_dim)/dynamic_slice | solution.py:62
  121.6 0.1 lt.47
  121.7 0.1 iota_compare_fusion
  121.8 5.7 %fusion.54 = (f32[32,8,2]{2,1,0:T(8,128)S(1)}, f32[32,8,2,64]{3,2,1,0:T(2,128)S(1)}) fusion(bf16[32,8,2,256]{3,2,1,0:T(2,128)(2,1)S(1)} %copy_dynamic-update-slice_fusion, bf16[32,8,64,256]{3,2,1,0:T(8,128)(2,1)} %bitcast.100, pred[32,64]{1,0:T(8,128)(4,1)S(1)} %iota_compare_fusion), kind=kOutput, calls=%fused_computation.72 | convolution fusion | flops 16875008 | bytes 8785920 | tf_op jit(solution)/shard_map/cond/branch_1_fun/nkgd,nksd->nkgs/dot_general | solution.py:38
  127.5 0.7 fusion.41
  128.3 0.2 copy.39
  128.4 4.9 %fusion.31 = bf16[32,8,2,256]{3,2,1,0:T(2,128)(2,1)S(1)} fusion(bf16[32,8,64,256]{3,2,1,0:T(8,128)(2,1)} %bitcast.101, f32[32,8,2]{2,1,0:T(8,128)S(1)} %get-tuple-element.113, f32[32,8,256]{2,1,0:T(8,128)S(1)} %copy.39, f32[32,8,2]{2,1,0:T(8,128)S(1)} %get-tuple-element.112, f32[32,8,2,64]{3,2,1,0:T(2,128)S(1)} %get-tuple-element.117, ...), kind=kOutput, calls=%fused_computation.23 | convolution fusion | flops 17367040 | bytes 9050112 | tf_op jit(solution)/shard_map/cond/branch_1_fun/nkgs,nksd->nkgd/dot_general | solution.py:46
  133.3 0.2 reshape.162
  133.5 12.0 %fusion.26 = bf16[32,3584]{1,0:T(8,128)(2,1)S(1)} fusion(bf16[32,4096]{1,0:T(8,128)(2,1)S(1)} %reshape.162, bf16[1,4096,3584]{2,1,0:T(8,128)(2,1)} %get-tuple-element.95, bf16[32,3584]{1,0:T(8,128)(2,1)S(1)} %get-tuple-element.88), kind=kOutput, calls=%fused_computation.18 | convolution fusion | flops 939868160 | bytes 30081024 | tf_op jit(solution)/shard_map/cond/branch_1_fun/dot_general | solution.py:49
  145.5 1.3 collective-permute-start
  146.8 0.0 copy-done.2
  146.9 3.1 %collective-permute-done = bf16[32,3584]{1,0:T(8,128)(2,1)S(1)} collective-permute-done((bf16[32,3584]{1,0:T(8,128)(2,1)S(1)}, bf16[32,3584]{1,0:T(8,128)(2,1)S(1)}, u32[]{:S(2)}, u32[]{:S(2)}) %collective-permute-start) | collective-permute-done | bytes 229408 | tf_op jit(solution)/shard_map/ppermute | solution.py:110
  150.0 0.2 fusion.50
  150.2 0.1 fusion.52
  150.3 16.3 %all_gather.3 = bf16[128,3584]{1,0:T(8,128)(2,1)S(1)} all-gather(bf16[32,3584]{1,0:T(8,128)(2,1)S(1)} %fusion.52), channel_id=1, replica_groups=mesh['inst'=1,'dev'=4,'side'=8] {'dev'}, dimensions={0}, use_global_device_ids=true | all-gather | bytes 1146880 | tf_op jit(solution)/shard_map/all_gather | solution.py:112
  166.6 1.4 conditional.3
  166.6 1.4 broadcast.103
  168.1 0.0 copy-start.1
  168.1 0.1 reduce-scatter.2.cloned.1.call-update
  168.1 61.4 %reduce-scatter.2.cloned.1.call-done = f32[32,3584]{1,0:T(8,128)} async-done(((f32[128,3584]{1,0:T(8,128)}), f32[32,3584]{1,0:T(8,128)}) %reduce-scatter.2.cloned.1.call-update) | async-done | bytes 458768 | tf_op jit(solution)/shard_map/reduce_scatter | solution.py:114
  229.5 1.1 fusion.53
  230.6 1.3 collective-permute-start.1
  231.9 5.8 %collective-permute-done.1 = bf16[16,3584]{1,0:T(8,128)(2,1)S(1)} collective-permute-done((bf16[16,3584]{1,0:T(8,128)(2,1)S(1)}, bf16[16,3584]{1,0:T(8,128)(2,1)S(1)}, u32[]{:S(2)}, u32[]{:S(2)}) %collective-permute-start.1) | collective-permute-done | bytes 114720 | tf_op jit(solution)/shard_map/ppermute | solution.py:119
  237.6 0.7 slice_select_fusion
  238.3 0.0 copy-done.1
  (14 shorter events, 0.3 us)
Async XLA Ops:
  6.5 1.2 copy-start
  6.6 222.9 %reduce-scatter.2.cloned.1.call-start = ((), (), s32[]{:S(2)}) async-start(), calls=%async_computation.1 | async-start | bytes 2293760 | tf_op jit(solution)/shard_map/reduce_scatter | solution.py:114
  7.7 139.1 %copy-start.2 = (f32[1,3584]{1,0:T(1,128)S(1)}, f32[1,3584]{1,0:T(1,128)}, u32[]{:S(2)}) copy-start(f32[1,3584]{1,0:T(1,128)} %param.24) | copy-start | bytes 43012
  44.7 13.9 %copy-start.3 = (s32[128]{0:T(128)S(1)}, s32[128]{0:T(128)}, u32[]{:S(2)}) copy-start(s32[128]{0:T(128)} %get-tuple-element.97) | copy-start | bytes 1540 | tf_op jit(solution)/shard_map/cond
  145.5 4.5 %collective-permute-start = (bf16[32,3584]{1,0:T(8,128)(2,1)S(1)}, bf16[32,3584]{1,0:T(8,128)(2,1)S(1)}, u32[]{:S(2)}, u32[]{:S(2)}) collective-permute-start(bf16[32,3584]{1,0:T(8,128)(2,1)S(1)} %get-tuple-element.120), channel_id=1, source_target_pairs={{0,4},{1,5},{2,6},{3,7},{8,12},{9,13},{10,14},{11,15},{16,20},{17,... | collective-permute-start | bytes 688136 | tf_op jit(solution)/shard_map/ppermute | solution.py:110
  168.1 70.2 %copy-start.1 = (bf16[128,3584]{1,0:T(8,128)(2,1)S(1)}, bf16[128,3584]{1,0:T(8,128)(2,1)}, u32[]{:S(2)}) copy-start(bf16[128,3584]{1,0:T(8,128)(2,1)} %param.16) | copy-start | bytes 2752516
  230.6 7.1 %collective-permute-start.1 = (bf16[16,3584]{1,0:T(8,128)(2,1)S(1)}, bf16[16,3584]{1,0:T(8,128)(2,1)S(1)}, u32[]{:S(2)}, u32[]{:S(2)}) collective-permute-start(bf16[16,3584]{1,0:T(8,128)(2,1)S(1)} %slice.39), channel_id=1, source_target_pairs={{4,0},{5,1},{6,2},{7,3},{12,8},{13,9},{14,10},{15,11},{20,16},{21,... | collective-permute-start | bytes 344072 | tf_op jit(solution)/shard_map/ppermute | solution.py:119
Sparse Core Ops, SparseCore 0:
  168.2 61.1 reduce-scatter.1
where the time goes:
time: 248 us; the launch traced here: 245 us
  local copies, waits for them, and re-layouts  87.4 us (35%)
  waiting for transfers between devices  70.3 us (28%)
  matrix products  50.8 us (20%)
  blocking collectives  16.3 us (7%)
  between operations  13.5 us (5%)
  other arithmetic  4.12 us (2%)
  starting transfers between devices  2.63 us (1%)
    another operation x3, local copies, waits for them, and re-layouts  73.4 us
    reduce_scatter x1, waiting for transfers between devices, device_fn(): summed = lax.psum_scatter(part_sum, 'dev', scatter_dimension=0, tiled=True)  61.4 us
    all_gather x1, blocking collectives, device_fn(): h_all = lax.all_gather(h_rows, 'dev', axis=0, tiled=True)  16.3 us
    dot_general x1, matrix products, attention_layer(): jnp.dot(normed, kv_weight, preferred_element_type=jnp.float32)  13.9 us
    dot_general x1, matrix products, attention_layer(): jnp.dot(normed, q_weight, preferred_element_type=jnp.float32)  13.9 us
    dot_general x1, matrix products, attention_layer(): attn_out = jnp.dot(mixed, o_weight, preferred_element_type=jnp.float32)  12 us
    dynamic_slice x3, local copies, waits for them, and re-layouts, pair_rows(): picked = lax.dynamic_index_in_dim(shaped, slot, axis=1, keepdims=False)  11.9 us
    ppermute x1, waiting for transfers between devices, device_fn(): back = lax.ppermute(x_ffn[:rows], 'side', to_attn)  5.76 us
  transfers between devices with their start and end apart: 3, of which 3 were waited for; matrix products, arithmetic and copies ran while one was open for 0% of the time, Pallas kernels for 0%

commit v1 on v0

v1 whole, which is shorter than its diff:
```python
import functools

import jax
import jax.numpy as jnp
import numpy as np
from jax import lax
from jax.experimental import pallas as pl
from jax.experimental.pallas import tpu as pltpu
from jax.sharding import PartitionSpec as P

EPS = 1e-5
ROPE_BASE = 10000.0
MESH = pl.DeviceIdType.MESH
F32 = jnp.float32
BF16 = jnp.bfloat16
COL = 256
CORES = 2
NEG = -1e30


def dot(lhs, rhs):
    return jnp.dot(lhs, rhs, preferred_element_type=F32)


def rms(rows, gain):
    rows_f = rows.astype(F32)
    inv = lax.rsqrt(jnp.mean(rows_f * rows_f, axis=-1, keepdims=True) + EPS)
    return (rows_f * inv * gain).astype(BF16)


def pair_blocks(first, second):
    rows, n = first.shape
    both = jnp.concatenate([first.reshape(rows // 8, 8, n), second.reshape(rows // 8, 8, n)], axis=1)
    return both.reshape(2 * rows, n)


def layer_kernel(n_dev, n_side,
                 x_hbm, len_hbm, freq_hbm, k_hbm, v_hbm, wq_hbm, wkv_hbm, wo_hbm, again_hbm, fgain_hbm,
                 wg_hbm, wu_hbm, wd_hbm, out_hbm,
                 act, lens, freqs, again, fgain, xres, wa, kbuf, vbuf, wo, wg, wu,
                 yb, qa, sb, pb, ob, osend, og, pp, precv, x1g, u, r1, r2, r3, fin, finr,
                 in_sem, w_sem, kv_sem, wo_sem, gu_sem, wd_sem, out_sem,
                 a2a_send, a2a_recv, pp_send, pp_recv, ag_send, ag_recv, u_send, u_recv,
                 rs_send, rs_recv, fin_send, fin_recv):
    dev = lax.axis_index('dev')
    side = lax.axis_index('side')
    n_x = n_side // CORES
    chip = lax.div(side, CORES)
    core = lax.rem(side, CORES)
    mate = {'side': CORES * chip + 1 - core}
    seqs, width = act.shape
    head = COL
    q_cols = osend.shape[1]
    half = width // 2
    rows = xres.shape[0]
    n_col = half // COL
    kv_half = wkv_hbm.shape[2] // 2
    prow, pcol = wa.shape[0], wa.shape[1]

    def on_x(r):
        return {'side': CORES * lax.rem(chip + r, n_x) + core}

    def on_y(r):
        return {'dev': lax.rem(dev + r + n_dev, n_dev)}

    barrier = pltpu.get_barrier_semaphore()
    peers = [mate] + [on_x(r) for r in range(1, n_x)] + [on_y(1), on_y(-1)]
    for peer in peers:
        pl.semaphore_signal(barrier, inc=1, device_id=peer, device_id_type=MESH)

    def cols(start, size):
        return pl.ds(pl.multiple_of(start, 128), size)

    def load(src, dst, sem, priority=1):
        pltpu.make_async_copy(src, dst, sem).start(priority=priority)

    def landed(dst, sem):
        pltpu.make_async_copy(dst, dst, sem).wait()

    mine = cols(core * half, half)
    other = cols((1 - core) * half, half)
    my_rows = pl.ds(pl.multiple_of(chip * rows, rows), rows)

    load(x_hbm, act, in_sem.at[0])
    load(len_hbm, lens, in_sem.at[1])
    load(freq_hbm, freqs, in_sem.at[2])
    load(again_hbm, again, in_sem.at[3])
    load(fgain_hbm, fgain, in_sem.at[4])
    load(x_hbm.at[my_rows, mine], xres, in_sem.at[5])

    def w_slot(j):
        return wa.at[:, :, j * COL:(j + 1) * COL]

    load(wq_hbm.at[:, :, cols(side * q_cols, COL)], w_slot(0), w_sem.at[0])
    load(wq_hbm.at[:, :, cols(side * q_cols + COL, COL)], w_slot(1), w_sem.at[1])
    load(wkv_hbm.at[:, :, cols(side * head, COL)], w_slot(2), w_sem.at[2])
    load(wkv_hbm.at[:, :, cols(kv_half + side * head, COL)], w_slot(3), w_sem.at[3])
    load(k_hbm.at[:, side], kbuf, kv_sem.at[0])
    load(v_hbm.at[:, side], vbuf, kv_sem.at[1])
    for r in range(n_x):
        src_chip = lax.rem(chip + n_x - r, n_x)
        load(wo_hbm.at[CORES * src_chip + core], wo.at[r], wo_sem.at[r])
    for j in range(n_col - 1):
        part = slice(j * COL, (j + 1) * COL)
        load(wg_hbm.at[:, :, cols(core * half + j * COL, COL)], wg.at[:, :, part], gu_sem.at[0, j])
        load(wu_hbm.at[:, :, cols(core * half + j * COL, COL)], wu.at[:, :, part], gu_sem.at[1, j])

    for i, ref in enumerate((act, lens, freqs, again, fgain, xres)):
        landed(ref, in_sem.at[i])
    row_id = lax.broadcasted_iota(jnp.int32, (seqs, seqs), 0)
    col_id = lax.broadcasted_iota(jnp.int32, (seqs, seqs), 1)
    wide = jnp.broadcast_to(lens[...].astype(F32), (seqs, seqs))
    len_col = jnp.sum(jnp.where(row_id == col_id, wide, 0.0), axis=1, keepdims=True)
    angle = len_col * freqs[...]
    cos_part = jnp.cos(angle)
    sin_part = jnp.sin(angle)

    def rotate(vecs):
        first, second = vecs[:, :head // 2], vecs[:, head // 2:]
        return jnp.concatenate([first * cos_part - second * sin_part, second * cos_part + first * sin_part], axis=1)

    @pl.loop(0, seqs // 16)
    def _(i):
        block = pl.ds(pl.multiple_of(i * 16, 16), 16)
        act[block, :] = rms(act[block, :], again[...])

    @pl.loop(0, 4)
    def _(j):
        landed(w_slot(0), w_sem.at[j])
        w = wa[:, :, cols(j * COL, COL)].reshape(prow * pcol, COL)
        yb[j] = dot(act[...], w)

    q0 = rotate(yb[0]).astype(BF16).astype(F32)
    q1 = rotate(yb[1]).astype(BF16).astype(F32)
    k_new = rotate(yb[2]).astype(BF16).astype(F32)
    v_new = yb[3].astype(BF16).astype(F32)
    qa[...] = pair_blocks(q0, q1).astype(BF16)
    scale = head ** -0.5
    self0 = jnp.sum(q0 * k_new, axis=1, keepdims=True)
    self1 = jnp.sum(q1 * k_new, axis=1, keepdims=True)
    self_score = pair_blocks(self0, self1) * scale
    len_rows = pair_blocks(len_col, len_col).astype(jnp.int32)

    span = kbuf.shape[1]
    keys = 8 * span
    landed(kbuf, kv_sem.at[0])
    for b in range(seqs // 8):
        k_blk = kbuf[8 * b:8 * b + 8].reshape(keys, head)
        sb[16 * b:16 * b + 16, :] = lax.dot_general(
            qa[16 * b:16 * b + 16, :], k_blk, (((1,), (1,)), ((), ())), preferred_element_type=F32)
    row = lax.broadcasted_iota(jnp.int32, (2 * seqs, keys), 0)
    key = lax.broadcasted_iota(jnp.int32, (2 * seqs, keys), 1)
    offset = key - lax.rem(row, 8) * span
    valid = (offset >= 0) & (offset < len_rows)
    scores = jnp.where(valid, sb[...] * scale, NEG)
    row_max = jnp.maximum(jnp.max(scores, axis=1, keepdims=True), self_score)
    exp_scores = jnp.exp(scores - row_max)
    self_exp = jnp.exp(self_score - row_max)
    total = jnp.sum(exp_scores, axis=1, keepdims=True) + self_exp
    pb[...] = exp_scores.astype(BF16)
    landed(vbuf, kv_sem.at[1])
    for b in range(seqs // 8):
        v_blk = vbuf[8 * b:8 * b + 8].reshape(keys, head)
        ob[16 * b:16 * b + 16, :] = dot(pb[16 * b:16 * b + 16, :], v_blk)
    mixed = ob[...] + self_exp.astype(BF16).astype(F32) * pair_blocks(v_new, v_new)
    mixed = (mixed / total).reshape(seqs // 8, 16, head)
    osend[:, :head] = mixed[:, :8].reshape(seqs, head).astype(BF16)
    osend[:, head:] = mixed[:, 8:].reshape(seqs, head).astype(BF16)

    last = (n_col - 1) * COL
    load(wg_hbm.at[:, :, cols(core * half + last, COL)], kbuf.at[0:prow], gu_sem.at[0, n_col - 1])
    load(wu_hbm.at[:, :, cols(core * half + last, COL)], vbuf.at[0:prow], gu_sem.at[1, n_col - 1])
    for j in range(n_col):
        load(wd_hbm.at[:, :, cols(core * half + j * COL, COL)], wa.at[:, :, j * COL:(j + 1) * COL], wd_sem.at[j])

    pl.semaphore_wait(barrier, len(peers))

    def send(src, dst, send_sem, recv_sem, where):
        pltpu.make_async_remote_copy(src, dst, send_sem, recv_sem, device_id=where, device_id_type=MESH).start()

    def arrived(dst, sem):
        pltpu.make_async_copy(dst, dst, sem).wait()

    for r in range(1, n_x):
        there = lax.rem(chip + r, n_x)
        send(osend.at[pl.ds(pl.multiple_of(there * rows, rows), rows)], og.at[r], a2a_send.at[r], a2a_recv.at[r], on_x(r))

    @pl.loop(0, 2 * n_col)
    def _(j):
        pp[j] = jnp.zeros_like(pp[0])

    steps = [0, 1] + [r for r in range(n_x - 1, 1, -1)]
    for r in steps:
        landed(wo.at[r], wo_sem.at[r])
        if r == 0:
            o_rows = osend[my_rows, :]
        else:
            arrived(og.at[r], a2a_recv.at[r])
            o_rows = og[r]

        def project(start):
            @pl.loop(0, n_col)
            def _(j, o_rows=o_rows, r=r):
                pp[start + j] += dot(o_rows, wo[r, :, cols((start + j) * COL, COL)])

        project((1 - core) * n_col)
        if r == steps[-1]:
            send(pp.at[pl.ds((1 - core) * n_col, n_col)], precv, pp_send.at[0], pp_recv.at[0], mate)
        project(core * n_col)
    arrived(precv, pp_recv.at[0])

    @pl.loop(0, n_col)
    def _(j):
        part = cols(j * COL, COL)
        full = cols(core * half + j * COL, COL)
        summed = pp[core * n_col + j] + precv[j]
        x1g[pl.ds(pl.multiple_of(dev * rows, rows), rows), full] = (xres[:, part].astype(F32) + summed).astype(BF16)

    def piece(owner, start, size):
        owner_rows = pl.ds(pl.multiple_of(lax.rem(owner + 2 * n_dev, n_dev) * rows, rows), rows)
        return x1g.at[owner_rows, cols(core * half + start, size)]

    def their_piece(owner, start, size):
        owner_rows = pl.ds(pl.multiple_of(lax.rem(owner + 2 * n_dev, n_dev) * rows, rows), rows)
        return x1g.at[owner_rows, cols((1 - core) * half + start, size)]

    quarter = half // 2
    own = piece(dev, 0, half)
    send(own, own, ag_send.at[0], ag_recv.at[0], on_y(1))
    send(own, own, ag_send.at[1], ag_recv.at[1], on_y(-1))
    send(own, own, ag_send.at[4], ag_recv.at[4], mate)
    below = piece(dev - 1, 0, half)
    arrived(below, ag_recv.at[0])
    below_a = piece(dev - 1, 0, quarter)
    send(below_a, below_a, ag_send.at[2], ag_recv.at[2], on_y(1))
    send(below, below, ag_send.at[5], ag_recv.at[5], mate)
    above = piece(dev + 1, 0, half)
    arrived(above, ag_recv.at[1])
    above_b = piece(dev + 1, quarter, quarter)
    send(above_b, above_b, ag_send.at[3], ag_recv.at[3], on_y(-1))
    send(above, above, ag_send.at[6], ag_recv.at[6], mate)
    far_a, far_b = piece(dev + 2, 0, quarter), piece(dev + 2, quarter, quarter)
    arrived(far_a, ag_recv.at[2])
    send(far_a, far_a, ag_send.at[7], ag_recv.at[7], mate)
    arrived(far_b, ag_recv.at[3])
    send(far_b, far_b, ag_send.at[8], ag_recv.at[8], mate)
    arrived(their_piece(dev, 0, half), ag_recv.at[4])
    arrived(their_piece(dev - 1, 0, half), ag_recv.at[5])
    arrived(their_piece(dev + 1, 0, half), ag_recv.at[6])
    arrived(their_piece(dev + 2, 0, quarter), ag_recv.at[7])
    arrived(their_piece(dev + 2, quarter, quarter), ag_recv.at[8])

    @pl.loop(0, seqs // 16)
    def _(i):
        block = pl.ds(pl.multiple_of(i * 16, 16), 16)
        act[block, :] = rms(x1g[block, :], fgain[...])

    def gated(j, gate_w, up_w):
        gate = dot(act[...], gate_w)
        up = dot(act[...], up_w)
        here = u.at[core * n_col + j]
        here[...] = (jax.nn.silu(gate) * up).astype(BF16)
        send(here, here, u_send.at[j], u_recv.at[j], mate)

    @pl.loop(0, n_col - 1)
    def _(j):
        landed(wg.at[:, :, 0:COL], gu_sem.at[0, j])
        landed(wu.at[:, :, 0:COL], gu_sem.at[1, j])
        part = cols(j * COL, COL)
        gated(j, wg[:, :, part].reshape(prow * pcol, COL), wu[:, :, part].reshape(prow * pcol, COL))

    landed(kbuf.at[0:prow], gu_sem.at[0, n_col - 1])
    landed(vbuf.at[0:prow], gu_sem.at[1, n_col - 1])
    gated(n_col - 1, kbuf[0:prow].reshape(prow * pcol, COL), vbuf[0:prow].reshape(prow * pcol, COL))
    for j in range(n_col):
        arrived(u.at[(1 - core) * n_col + j], u_recv.at[j])

    def way(j):
        sign = (1 - 2 * core) * (1 - 2 * lax.rem(j, 2))
        return sign

    def rows_of(owner):
        return pl.ds(pl.multiple_of(lax.rem(owner + 2 * n_dev, n_dev) * rows, rows), rows)

    @pl.loop(0, n_col)
    def _(j):
        landed(wa.at[:, :, 0:COL], wd_sem.at[j])
        total_y = jnp.zeros((seqs, COL), F32)
        down = wa.at[:, :, cols(j * COL, COL)]
        full_u = jnp.concatenate([u[i] for i in range(2 * n_col)], axis=1)
        yb[j] = dot(full_u, down[...].reshape(prow * pcol, COL)) + total_y
        sign = way(j)
        send(yb.at[j, rows_of(dev + 2)], r1.at[j], rs_send.at[0, j], rs_recv.at[0, j], on_y(sign))
        send(yb.at[j, rows_of(dev - sign)], r3.at[j], rs_send.at[2, j], rs_recv.at[2, j], on_y(-sign))

    @pl.loop(0, n_col)
    def _(j):
        sign = way(j)
        arrived(r1.at[j], rs_recv.at[0, j])
        yb[j, rows_of(dev + sign), :] += r1[j]
        send(yb.at[j, rows_of(dev + sign)], r2.at[j], rs_send.at[1, j], rs_recv.at[1, j], on_y(sign))

    @pl.loop(0, n_col)
    def _(j):
        arrived(r2.at[j], rs_recv.at[1, j])
        arrived(r3.at[j], rs_recv.at[2, j])
        y = (yb[j, rows_of(dev), :] + r2[j] + r3[j]).astype(BF16)
        x1 = x1g[rows_of(dev), cols(core * half + j * COL, COL)]
        fin[:, cols(j * COL, COL)] = (x1.astype(F32) + y.astype(F32)).astype(BF16)

    blk = rows // CORES
    my_blk = pl.ds(pl.multiple_of(core * blk, blk), blk)
    mate_blk = pl.ds(pl.multiple_of((1 - core) * blk, blk), blk)
    send(fin.at[mate_blk], finr, fin_send.at[0], fin_recv.at[0], mate)
    store = pltpu.make_async_copy(fin.at[my_blk], out_hbm.at[:, mine], out_sem.at[0])
    store.start()
    arrived(finr, fin_recv.at[0])
    store2 = pltpu.make_async_copy(finr, out_hbm.at[:, other], out_sem.at[1])
    store2.start()

    for r in range(1, n_x):
        arrived(og.at[r], a2a_send.at[r])
    arrived(precv, pp_send.at[0])
    for i, ref in enumerate((own, own, below_a, above_b, own, below, above, far_a, far_b)):
        arrived(ref, ag_send.at[i])
    for j in range(n_col):
        arrived(u.at[0], u_send.at[j])
        for i in range(3):
            arrived(r1.at[0], rs_send.at[i, j])
    arrived(finr, fin_send.at[0])
    store.wait()
    store2.wait()


def solution(mesh):
    n_side = mesh.shape['side']
    n_dev = mesh.shape['dev']
    batch_axes = ('inst', 'dev')
    in_specs = (
        P(batch_axes, None),
        P(batch_axes),
        P(None, batch_axes, None, None, None),
        P(None, batch_axes, None, None, None),
        P(), P(), P(), P(), P(),
        P(None, None, 'dev'),
        P(None, None, 'dev'),
        P(None, 'dev', None),
    )
    out_specs = P(('inst', 'dev', 'side'), None)

    def device_fn(hidden, cache_len, k_cache, v_cache, w_q, w_kv, w_o, attn_gain, ffn_gain, w_gate, w_up, w_down):
        seqs, width = hidden.shape
        span, head = k_cache.shape[3:]
        ff = w_gate.shape[2]
        half = width // 2
        rows = seqs * CORES // n_side
        n_x = n_side // CORES
        n_col = half // COL
        q_cols = w_q.shape[2] // n_side
        tall = width // span
        freqs = jnp.asarray(ROPE_BASE ** (-np.arange(head // 2, dtype=np.float64) / (head // 2)), F32)[None]

        def fold(w):
            return w.reshape(w.shape[1] // span, span, w.shape[2])

        args = (hidden, cache_len.reshape(1, seqs), freqs, k_cache[0], v_cache[0], fold(w_q), fold(w_kv),
                w_o.reshape(n_side, w_o.shape[1] // n_side, width), attn_gain, ffn_gain,
                fold(w_gate), fold(w_up), fold(w_down))
        vmem = pltpu.VMEM
        dma = pltpu.SemaphoreType.DMA
        scratch = [
            vmem((seqs, width), BF16), vmem((1, seqs), jnp.int32), vmem((1, head // 2), F32),
            vmem((1, width), F32), vmem((1, width), F32), vmem((rows, half), BF16),
            vmem((tall, span, half), BF16),
            vmem((seqs, span, head), BF16), vmem((seqs, span, head), BF16),
            vmem((n_x, q_cols, width), BF16),
            vmem((tall, span, ff // 2 - COL), BF16), vmem((tall, span, ff // 2 - COL), BF16),
            vmem((n_col, seqs, COL), F32), vmem((2 * seqs, head), BF16),
            vmem((2 * seqs, 8 * span), F32), vmem((2 * seqs, 8 * span), BF16), vmem((2 * seqs, head), F32),
            vmem((seqs, q_cols), BF16), vmem((n_x, rows, q_cols), BF16),
            vmem((2 * n_col, rows, COL), F32), vmem((n_col, rows, COL), F32),
            vmem((n_dev * rows, width), BF16), vmem((2 * n_col, seqs, COL), BF16),
            vmem((n_col, rows, COL), F32), vmem((n_col, rows, COL), F32), vmem((n_col, rows, COL), F32),
            vmem((rows, half), BF16), vmem((rows // CORES, half), BF16),
            dma((6,)), dma((4,)), dma((2,)), dma((n_x,)), dma((2, n_col)), dma((n_col,)), dma((2,)),
            dma((n_x,)), dma((n_x,)), dma((1,)), dma((1,)), dma((9,)), dma((9,)), dma((n_col,)), dma((n_col,)),
            dma((3, n_col)), dma((3, n_col)), dma((1,)), dma((1,)),
        ]
        anywhere = pl.BlockSpec(memory_space=pl.ANY)
        return pl.pallas_call(
            functools.partial(layer_kernel, n_dev, n_side),
            out_shape=jax.ShapeDtypeStruct((rows // CORES, width), BF16),
            in_specs=[anywhere] * len(args),
            out_specs=anywhere,
            scratch_shapes=scratch,
            compiler_params=pltpu.CompilerParams(
                collective_id=0, has_side_effects=True, vmem_limit_bytes=67_043_328),
        )(*args)

    return jax.shard_map(device_fn, mesh=mesh, in_specs=in_specs, out_specs=out_specs, check_vma=False)
```

time: 248 us -> 66 us (0.27); the launches traced: 245 us -> 65.9 us
  local copies, waits for them, and re-layouts: 87.4 us -> 1.55 us
  waiting for transfers between devices: 70.3 us -> 0 us
  Pallas kernels: 0 us -> 64.4 us
  matrix products: 50.8 us -> 0 us
  blocking collectives: 16.3 us -> 0 us
  between operations: 13.5 us -> 0.01 us
  other arithmetic: 4.12 us -> 0 us
  starting transfers between devices: 2.63 us -> 0 us
    another operation x3 -> x0, local copies, waits for them, and re-layouts: 73.4 us -> none
    pallas_call x0 -> x1, Pallas kernels: none -> 64.4 us  [device_fn(): pl.pallas_call(functools.partial(layer_kernel, n_dev, n_side), out_shape=...]
    reduce_scatter x1 -> x0, waiting for transfers between devices: 61.4 us -> none  [device_fn(): summed = lax.psum_scatter(part_sum, 'dev', scatter_dimension=0, tiled=True)]
    dot_general x6 -> x0, matrix products: 50.8 us -> none  [the longest x1 13.9 us: attention_layer(): jnp.dot(normed, kv_weight, preferred_element_type=jnp.float32)]
    all_gather x1 -> x0, blocking collectives: 16.3 us -> none  [device_fn(): h_all = lax.all_gather(h_rows, 'dev', axis=0, tiled=True)]
    dynamic_slice x3 -> x0, local copies, waits for them, and re-layouts: 11.9 us -> none  [pair_rows(): picked = lax.dynamic_index_in_dim(shaped, slot, axis=1, keepdims=False)]
    ppermute x2 -> x0, waiting for transfers between devices: 8.86 us -> none  [the longest x1 5.76 us: device_fn(): back = lax.ppermute(x_ffn[:rows], 'side', to_attn)]
    ppermute x2 -> x0, starting transfers between devices: 2.63 us -> none  [the longest x1 1.32 us: device_fn(): sent = lax.ppermute(x_pair, 'side', to_ffn)]
  transfers between devices with their start and end apart: 3 -> 0, of which waited for: 3 -> 0; matrix products, arithmetic and copies ran while one was open for 0% -> 0% of each run, Pallas kernels for 0% -> 0%
where the time goes in v1:
time: 66 us; the launch traced here: 65.9 us
  Pallas kernels  64.4 us (98%)
  local copies, waits for them, and re-layouts  1.55 us (2%)
    pallas_call x1, Pallas kernels, device_fn(): pl.pallas_call(functools.partial(layer_kernel, n_dev, n_side), out_shape=...  64.4 us
    unnamed x1, local copies, waits for them, and re-layouts  1.55 us

profile of v1, /device:TPU:97, one launch (start us, length us, event | category | flops | bytes accessed | tf_op | source)
XLA Modules:
  0.0 65.9 jit_solution(18231240645218764908)
XLA Ops:
  0.0 64.4 %shard_map.127 = bf16[16,3584]{1,0:T(8,128)(2,1)} custom-call(bf16[128,3584]{1,0:T(8,128)(2,1)} %x_hbm.1, s32[1,128]{1,0:T(1,128)} %bitcast.17, f32[1,128]{1,0:T(1,128)} %constant.3.freq_hbm, bf16[128,8,64,256]{3,2,1,0:T(8,128)(2,1)} %bitcast.9, bf16[128,8,64,256]{3,2,1,0:T(8,128)(2,1)} %bitcast.10, bf16[56,64,4096]{2,1,0:T(8,128)(2,1)} %bitcast.11, ...), custom_call_target="tpu_custom_call" | custom-call | tf_op jit(solution)/shard_map/pallas_call | solution.py:390
  64.4 1.6 %copy.15 = bf16[16,3584]{1,0:T(8,128)(2,1)} copy(bf16[16,3584]{1,0:T(8,128)(2,1)} %shard_map.127) | data formatting | bytes 229376

commit v2 on v1

v2 whole, which is shorter than its diff:
```python
import functools

import jax
import jax.numpy as jnp
import numpy as np
from jax import lax
from jax.experimental import pallas as pl
from jax.experimental.pallas import tpu as pltpu
from jax.sharding import PartitionSpec as P

EPS = 1e-5
ROPE_BASE = 10000.0
MESH = pl.DeviceIdType.MESH
F32 = jnp.float32
BF16 = jnp.bfloat16
COL = 256
CORES = 2
NEG = -1e30


def dot(lhs, rhs):
    return jnp.dot(lhs, rhs, preferred_element_type=F32)


def rms_scale(square_sum, width):
    return lax.rsqrt(square_sum / width + EPS)


def square_sums(parts):
    acc = None
    for part in parts:
        for g in range(part.shape[1] // 128):
            x = part[:, g * 128:(g + 1) * 128]
            acc = x * x if acc is None else acc + x * x
    return jnp.sum(acc, axis=1, keepdims=True)


def pair_blocks(first, second):
    rows, n = first.shape
    both = jnp.concatenate([first.reshape(rows // 8, 8, n), second.reshape(rows // 8, 8, n)], axis=1)
    return both.reshape(2 * rows, n)


class Phases:
    def __init__(self):
        self.scope = None

    def __call__(self, name):
        if self.scope is not None:
            self.scope.__exit__(None, None, None)
        self.scope = None if name is None else jax.named_scope(name)
        if self.scope is not None:
            self.scope.__enter__()


def layer_kernel(n_dev, n_side,
                 x_hbm, len_hbm, freq_hbm, k_hbm, v_hbm, wq_hbm, wkv_hbm, wo_hbm, again_hbm, fgain_hbm,
                 wg_hbm, wu_hbm, wd_hbm, out_hbm,
                 act, lens, freqs, again, fgain, xres, wa, kbuf, vbuf, wo, wg, wu,
                 yb, ub, qa, sb, pb, ob, osend, og, pp, precv, x1b, hg, u, r1, r2, r3, fin,
                 in_sem, w_sem, kv_sem, wo_sem, gu_sem, tail_sem, wd_sem, out_sem,
                 a2a_send, a2a_recv, pp_send, pp_recv, ag_send, ag_recv, u_send, u_recv,
                 rs_send, rs_recv, fin_send, fin_recv):
    dev = lax.axis_index('dev')
    side = lax.axis_index('side')
    n_x = n_side // CORES
    chip = lax.div(side, CORES)
    core = lax.rem(side, CORES)
    mate = {'side': CORES * chip + 1 - core}
    seqs, width = act.shape
    head = COL
    q_cols = osend.shape[1]
    half = width // 2
    rows = xres.shape[0]
    n_col = half // COL
    kq = (n_col + 1) // 2 * COL // wa.shape[1]
    n_main = wg.shape[2] // COL
    n_tail = n_col - n_main
    kv_half = wkv_hbm.shape[2] // 2
    prow, pcol = wa.shape[0], wa.shape[1]

    def on_x(r):
        return {'side': CORES * lax.rem(chip + r, n_x) + core}

    def on_y(r):
        return {'dev': lax.rem(dev + r + n_dev, n_dev)}

    phase = Phases()
    phase('start')
    barrier = pltpu.get_barrier_semaphore()
    peers = [mate] + [on_x(r) for r in range(1, n_x)] + [on_y(1), on_y(-1)]
    for peer in peers:
        pl.semaphore_signal(barrier, inc=1, device_id=peer, device_id_type=MESH)

    def cols(start, size):
        return pl.ds(pl.multiple_of(start, 128), size)

    def load(src, dst, sem, priority=1):
        pltpu.make_async_copy(src, dst, sem).start(priority=priority)

    def landed(dst, sem):
        pltpu.make_async_copy(dst, dst, sem).wait()

    mine = cols(core * half, half)
    other = cols((1 - core) * half, half)
    my_rows = pl.ds(pl.multiple_of(chip * rows, rows), rows)

    load(x_hbm, act, in_sem.at[0], 0)
    load(len_hbm, lens, in_sem.at[1], 0)
    load(freq_hbm, freqs, in_sem.at[2], 0)
    load(again_hbm, again, in_sem.at[3], 0)
    load(fgain_hbm, fgain, in_sem.at[4], 0)
    load(x_hbm.at[my_rows], xres, in_sem.at[5], 0)

    def w_slot(j):
        return wa.at[:, :, j * COL:(j + 1) * COL]

    load(wq_hbm.at[:, :, cols(side * q_cols, COL)], w_slot(0), w_sem.at[0], 0)
    load(wq_hbm.at[:, :, cols(side * q_cols + COL, COL)], w_slot(1), w_sem.at[1], 0)
    load(wkv_hbm.at[:, :, cols(side * head, COL)], w_slot(2), w_sem.at[2], 0)
    load(wkv_hbm.at[:, :, cols(kv_half + side * head, COL)], w_slot(3), w_sem.at[3], 0)
    phase('wait_x')
    for i, ref in enumerate((act, lens, freqs, again, fgain, xres)):
        landed(ref, in_sem.at[i])
    load(k_hbm.at[:, side], kbuf, kv_sem.at[0], 0)
    load(v_hbm.at[:, side], vbuf, kv_sem.at[1], 0)
    for r in range(n_x):
        src_chip = lax.rem(chip + n_x - r, n_x)
        load(wo_hbm.at[CORES * src_chip + core], wo.at[r], wo_sem.at[r])
    phase('tables')
    row_id = lax.broadcasted_iota(jnp.int32, (seqs, seqs), 0)
    col_id = lax.broadcasted_iota(jnp.int32, (seqs, seqs), 1)
    wide = jnp.broadcast_to(lens[...].astype(F32), (seqs, seqs))
    len_col = jnp.sum(jnp.where(row_id == col_id, wide, 0.0), axis=1, keepdims=True)
    angle = len_col * freqs[...]
    cos_part = jnp.cos(angle)
    sin_part = jnp.sin(angle)

    def rotate(vecs):
        first, second = vecs[:, :head // 2], vecs[:, head // 2:]
        return jnp.concatenate([first * cos_part - second * sin_part, second * cos_part + first * sin_part], axis=1)

    phase('norm1')
    inv = rms_scale(square_sums([act[:, i * COL:(i + 1) * COL].astype(F32) for i in range(2 * n_col)]), width)
    for i in range(2 * n_col):
        part = slice(i * COL, (i + 1) * COL)
        act[:, part] = (act[:, part].astype(F32) * inv * again[:, part]).astype(BF16)

    phase('qkv')
    @pl.loop(0, 4)
    def _(j):
        landed(w_slot(0), w_sem.at[j])
        w = wa[:, :, cols(j * COL, COL)].reshape(prow * pcol, COL)
        yb[j] = dot(act[...], w)

    phase('rope')
    q0 = rotate(yb[0]).astype(BF16).astype(F32)
    q1 = rotate(yb[1]).astype(BF16).astype(F32)
    k_new = rotate(yb[2]).astype(BF16).astype(F32)
    v_new = yb[3].astype(BF16).astype(F32)
    qa[...] = pair_blocks(q0, q1).astype(BF16)
    scale = head ** -0.5
    self0 = jnp.sum(q0 * k_new, axis=1, keepdims=True)
    self1 = jnp.sum(q1 * k_new, axis=1, keepdims=True)
    self_score = pair_blocks(self0, self1) * scale
    len_rows = pair_blocks(len_col, len_col).astype(jnp.int32)

    span = kbuf.shape[1]
    keys = 8 * span
    phase('wait_k')
    landed(kbuf, kv_sem.at[0])
    phase('scores')
    for b in range(seqs // 8):
        k_blk = kbuf[8 * b:8 * b + 8].reshape(keys, head)
        sb[16 * b:16 * b + 16, :] = lax.dot_general(
            qa[16 * b:16 * b + 16, :], k_blk, (((1,), (1,)), ((), ())), preferred_element_type=F32)
    phase('softmax')
    row = lax.broadcasted_iota(jnp.int32, (2 * seqs, keys), 0)
    key = lax.broadcasted_iota(jnp.int32, (2 * seqs, keys), 1)
    offset = key - lax.rem(row, 8) * span
    valid = (offset >= 0) & (offset < len_rows)
    scores = jnp.where(valid, sb[...] * scale, NEG)
    row_max = jnp.maximum(jnp.max(scores, axis=1, keepdims=True), self_score)
    exp_scores = jnp.exp(scores - row_max)
    self_exp = jnp.exp(self_score - row_max)
    total = jnp.sum(exp_scores, axis=1, keepdims=True) + self_exp
    pb[...] = exp_scores.astype(BF16)
    phase('wait_v')
    landed(vbuf, kv_sem.at[1])
    phase('mix')
    for b in range(seqs // 8):
        v_blk = vbuf[8 * b:8 * b + 8].reshape(keys, head)
        ob[16 * b:16 * b + 16, :] = dot(pb[16 * b:16 * b + 16, :], v_blk)
    mixed = ob[...] + self_exp.astype(BF16).astype(F32) * pair_blocks(v_new, v_new)
    mixed = (mixed / total).reshape(seqs // 8, 16, head)
    osend[:, :head] = mixed[:, :8].reshape(seqs, head).astype(BF16)
    osend[:, head:] = mixed[:, 8:].reshape(seqs, head).astype(BF16)

    phase('loads2')
    seg = ((0, kq), (half // pcol, kq), (kq, half // pcol - kq), (half // pcol + kq, half // pcol - kq))

    def load_gate_up(part):
        for i in (2 * part, 2 * part + 1):
            first, count = seg[i]
            at = pl.ds(first, count)
            for m, (w_hbm, w_buf, tail) in enumerate(((wg_hbm, wg, kbuf), (wu_hbm, wu, vbuf))):
                load(w_hbm.at[at, :, cols(core * half, n_main * COL)], w_buf.at[at], gu_sem.at[m, i])
                for t in range(n_tail):
                    load(w_hbm.at[at, :, cols(core * half + (n_main + t) * COL, COL)],
                         tail.at[pl.ds(t * prow + first, count)], tail_sem.at[m, t, i])

    load_gate_up(0)
    load_gate_up(1)
    phase('a2a_start')
    pl.semaphore_wait(barrier, len(peers))

    def send(src, dst, send_sem, recv_sem, where):
        pltpu.make_async_remote_copy(src, dst, send_sem, recv_sem, device_id=where, device_id_type=MESH).start()

    def arrived(dst, sem):
        pltpu.make_async_copy(dst, dst, sem).wait()

    for r in range(1, n_x):
        there = lax.rem(chip + r, n_x)
        send(osend.at[pl.ds(pl.multiple_of(there * rows, rows), rows)], og.at[r], a2a_send.at[r], a2a_recv.at[r], on_x(r))

    phase('proj')
    steps = [0, 1] + [r for r in range(n_x - 1, 1, -1)]
    for r in steps[:-1]:
        landed(wo.at[r], wo_sem.at[r])
        if r == 0:
            pp[...] = dot(osend[my_rows, :], wo[0])
        else:
            arrived(og.at[r], a2a_recv.at[r])
            pp[...] += dot(og[r], wo[r])
    r = steps[-1]
    landed(wo.at[r], wo_sem.at[r])
    arrived(og.at[r], a2a_recv.at[r])
    for i in range(2):
        part = slice(i * half, (i + 1) * half)
        pp[:, part] += dot(og[r], wo[r, :, part])
        send(pp.at[:, part], precv.at[:, part], pp_send.at[i], pp_recv.at[i], mate)
    for j in range(n_col):
        load(wd_hbm.at[:, :, cols(core * half + j * COL, COL)], wa.at[:, :, j * COL:(j + 1) * COL], wd_sem.at[j])

    phase('wait_mate')
    dev_rows = pl.ds(pl.multiple_of(dev * rows, rows), rows)
    for i in range(2):
        part = slice(i * half, (i + 1) * half)
        arrived(precv.at[:, part], pp_recv.at[i])
        x1b[:, part] = (xres[:, part].astype(F32) + (pp[:, part] + precv[:, part])).astype(BF16)
    phase('norm2')
    inv2 = rms_scale(square_sums([x1b[:, i * COL:(i + 1) * COL].astype(F32) for i in range(2 * n_col)]), width)
    for i in range(2 * n_col):
        part = slice(i * COL, (i + 1) * COL)
        hg[dev_rows, part] = (x1b[:, part].astype(F32) * inv2 * fgain[:, part]).astype(BF16)

    phase('gather')
    ka = kq * pcol // 2
    kb = (half - kq * pcol) // 2
    strips = (((0, ka), (ka, ka)), ((2 * ka, kb), (2 * ka + kb, kb)))

    def piece(owner, strip, whose):
        owner_rows = pl.ds(pl.multiple_of(lax.rem(owner + 2 * n_dev, n_dev) * rows, rows), rows)
        return hg.at[owner_rows, cols(whose * half + strip[0], strip[1])]

    def hop(owner, strip, p, i, where):
        ref = piece(owner, strip, core)
        send(ref, ref, ag_send.at[p, i], ag_recv.at[p, i], where)

    def came(owner, strip, p, i):
        arrived(piece(owner, strip, core), ag_recv.at[p, i])

    source = ((-1, 0), (1, 1), (-1, 1), (1, 0), (2, 0), (2, 1))
    for p in range(2):
        hop(dev, strips[p][0], p, 0, on_y(1))
        hop(dev, strips[p][1], p, 1, on_y(-1))
        hop(dev, strips[p][1], p, 2, on_y(1))
        hop(dev, strips[p][0], p, 3, on_y(-1))

    def take(p, i):
        owner, strip = dev + source[i][0], strips[p][source[i][1]]
        came(owner, strip, p, i)
        if i < 2:
            hop(owner, strip, p, 4 + i, on_y(1 - 2 * i))
        hop(owner, strip, p, 6 + i, mate)

    def from_mate(p):
        for i in range(6):
            owner, strip = dev + source[i][0], strips[p][source[i][1]]
            arrived(piece(owner, strip, 1 - core), ag_recv.at[p, 6 + i])

    def weights(m, j, i):
        first, count = seg[i]
        main, tail = (wg, kbuf) if m == 0 else (wu, vbuf)
        if isinstance(j, int) and j >= n_main:
            start = (j - n_main) * prow + first
            return tail[start:start + count].reshape(count * pcol, COL)
        return main[first:first + count, :, cols(j * COL, COL)].reshape(count * pcol, COL)

    def partial_sum(m, j, p):
        out = None
        for i in (2 * p, 2 * p + 1):
            first, count = seg[i]
            term = dot(hg[:, first * pcol:(first + count) * pcol], weights(m, j, i))
            out = term if out is None else out + term
        return out

    def gate_up(p, j):
        gate, up = partial_sum(0, j, p), partial_sum(1, j, p)
        if p == 0:
            yb[j] = gate
            ub[j] = up
        else:
            here = u.at[core * n_col + j]
            here[...] = (jax.nn.silu(yb[j] + gate) * (ub[j] + up)).astype(BF16)
            send(here, here, u_send.at[j], u_recv.at[j], mate)

    def gate_up_part(p):
        for i in (2 * p, 2 * p + 1):
            first, count = seg[i]
            for m, (w_buf, tail) in enumerate(((wg, kbuf), (wu, vbuf))):
                landed(w_buf.at[pl.ds(first, count)], gu_sem.at[m, i])
                for t in range(n_tail):
                    landed(tail.at[pl.ds(t * prow + first, count)], tail_sem.at[m, t, i])
        phase('gateup%d' % p)

        @pl.loop(0, n_main)
        def _(j):
            gate_up(p, j)

        for t in range(n_tail):
            gate_up(p, n_main + t)

    for p, i in ((0, 0), (0, 1), (0, 2), (0, 3), (1, 0), (1, 1), (0, 4), (0, 5), (1, 2), (1, 3)):
        take(p, i)
    from_mate(0)
    phase('wait_gu0')
    gate_up_part(0)
    phase('gather2')
    take(1, 4)
    take(1, 5)
    from_mate(1)
    phase('wait_gu1')
    gate_up_part(1)
    phase('down0')
    ahead = 3
    fold_half = half // pcol

    def u_half(whose):
        return jnp.concatenate([u[whose * n_col + i] for i in range(n_col)], axis=1)

    def down_half(whose, j):
        at = pl.ds(whose * fold_half, fold_half)
        return dot(u_half(whose), wa[at, :, cols(j * COL, COL)].reshape(half, COL))

    @pl.loop(0, ahead)
    def _(j):
        landed(wa.at[:, :, 0:COL], wd_sem.at[j])
        yb[j] = down_half(core, j)

    phase('wait_u')
    for j in range(n_col):
        arrived(u.at[(1 - core) * n_col + j], u_recv.at[j])

    phase('down')
    def way(j):
        sign = (1 - 2 * core) * (1 - 2 * lax.rem(j, 2))
        return sign

    def rows_of(owner):
        return pl.ds(pl.multiple_of(lax.rem(owner + 2 * n_dev, n_dev) * rows, rows), rows)

    def pass_on(j):
        sign = way(j)
        send(yb.at[j, rows_of(dev + 2)], r1.at[j], rs_send.at[0, j], rs_recv.at[0, j], on_y(sign))
        send(yb.at[j, rows_of(dev - sign)], r3.at[j], rs_send.at[2, j], rs_recv.at[2, j], on_y(-sign))

    @pl.loop(0, ahead)
    def _(j):
        yb[j] += down_half(1 - core, j)
        pass_on(j)

    @pl.loop(ahead, n_col)
    def _(j):
        landed(wa.at[:, :, 0:COL], wd_sem.at[j])
        yb[j] = dot(jnp.concatenate([u[i] for i in range(2 * n_col)], axis=1),
                    wa[:, :, cols(j * COL, COL)].reshape(prow * pcol, COL))
        pass_on(j)

    phase('stage2')
    @pl.loop(0, n_col)
    def _(j):
        sign = way(j)
        arrived(r1.at[j], rs_recv.at[0, j])
        yb[j, rows_of(dev + sign), :] += r1[j]
        send(yb.at[j, rows_of(dev + sign)], r2.at[j], rs_send.at[1, j], rs_recv.at[1, j], on_y(sign))

    phase('final')
    @pl.loop(0, n_col)
    def _(j):
        arrived(r2.at[j], rs_recv.at[1, j])
        arrived(r3.at[j], rs_recv.at[2, j])
        y = (yb[j, rows_of(dev), :] + r2[j] + r3[j]).astype(BF16)
        x1 = x1b[:, cols(core * half + j * COL, COL)]
        fin[:, cols(j * COL, COL)] = (x1.astype(F32) + y.astype(F32)).astype(BF16)

    phase('fin')
    blk = rows // CORES
    my_blk = pl.ds(pl.multiple_of(core * blk, blk), blk)
    mate_blk = pl.ds(pl.multiple_of((1 - core) * blk, blk), blk)
    send(fin.at[mate_blk], out_hbm.at[:, mine], fin_send.at[0], fin_recv.at[0], mate)
    store = pltpu.make_async_copy(fin.at[my_blk], out_hbm.at[:, mine], out_sem.at[0])
    store.start()
    arrived(out_hbm.at[:, other], fin_recv.at[0])
    phase('drain')
    for r in range(1, n_x):
        arrived(og.at[r], a2a_send.at[r])
    for i in range(2):
        part = slice(i * half, (i + 1) * half)
        arrived(precv.at[:, part], pp_send.at[i])
    for p in range(2):
        for i in range(12):
            strip = strips[p][(0, 1, 1, 0, 0, 1, 0, 1, 1, 0, 0, 1)[i]]
            arrived(piece(dev, strip, core), ag_send.at[p, i])
    for j in range(n_col):
        arrived(u.at[0], u_send.at[j])
        for i in range(3):
            arrived(r1.at[0], rs_send.at[i, j])
    arrived(fin.at[mate_blk], fin_send.at[0])
    store.wait()
    phase(None)


def solution(mesh):
    n_side = mesh.shape['side']
    n_dev = mesh.shape['dev']
    batch_axes = ('inst', 'dev')
    in_specs = (
        P(batch_axes, None),
        P(batch_axes),
        P(None, batch_axes, None, None, None),
        P(None, batch_axes, None, None, None),
        P(), P(), P(), P(), P(),
        P(None, None, 'dev'),
        P(None, None, 'dev'),
        P(None, 'dev', None),
    )
    out_specs = P(('inst', 'dev', 'side'), None)

    def device_fn(hidden, cache_len, k_cache, v_cache, w_q, w_kv, w_o, attn_gain, ffn_gain, w_gate, w_up, w_down):
        seqs, width = hidden.shape
        span, head = k_cache.shape[3:]
        ff = w_gate.shape[2]
        half = width // 2
        rows = seqs * CORES // n_side
        n_x = n_side // CORES
        n_col = half // COL
        q_cols = w_q.shape[2] // n_side
        tall = width // span
        freqs = jnp.asarray(ROPE_BASE ** (-np.arange(head // 2, dtype=np.float64) / (head // 2)), F32)[None]

        def fold(w):
            return w.reshape(w.shape[1] // span, span, w.shape[2])

        args = (hidden, cache_len.reshape(1, seqs), freqs, k_cache[0], v_cache[0], fold(w_q), fold(w_kv),
                w_o.reshape(n_side, w_o.shape[1] // n_side, width), attn_gain, ffn_gain,
                fold(w_gate), fold(w_up), fold(w_down))
        vmem = pltpu.VMEM
        dma = pltpu.SemaphoreType.DMA
        main = ff // CORES - 2 * COL
        scratch = [
            vmem((seqs, width), BF16), vmem((1, seqs), jnp.int32), vmem((1, head // 2), F32),
            vmem((1, width), F32), vmem((1, width), F32), vmem((rows, width), BF16),
            vmem((tall, span, half), BF16),
            vmem((seqs, span, head), BF16), vmem((seqs, span, head), BF16),
            vmem((n_x, q_cols, width), BF16),
            vmem((tall, span, main), BF16), vmem((tall, span, main), BF16),
            vmem((n_col, seqs, COL), F32), vmem((n_col, seqs, COL), F32), vmem((2 * seqs, head), BF16),
            vmem((2 * seqs, 8 * span), F32), vmem((2 * seqs, 8 * span), BF16), vmem((2 * seqs, head), F32),
            vmem((seqs, q_cols), BF16), vmem((n_x, rows, q_cols), BF16),
            vmem((rows, width), F32), vmem((rows, width), F32), vmem((rows, width), BF16),
            vmem((n_dev * rows, width), BF16), vmem((2 * n_col, seqs, COL), BF16),
            vmem((n_col, rows, COL), F32), vmem((n_col, rows, COL), F32), vmem((n_col, rows, COL), F32),
            vmem((rows, half), BF16),
            dma((6,)), dma((4,)), dma((2,)), dma((n_x,)), dma((2, 4)), dma((2, 2, 4)), dma((n_col,)), dma((1,)),
            dma((n_x,)), dma((n_x,)), dma((2,)), dma((2,)), dma((2, 12)), dma((2, 12)), dma((n_col,)), dma((n_col,)),
            dma((3, n_col)), dma((3, n_col)), dma((1,)), dma((1,)),
        ]
        anywhere = pl.BlockSpec(memory_space=pl.ANY)
        return pl.pallas_call(
            functools.partial(layer_kernel, n_dev, n_side),
            out_shape=jax.ShapeDtypeStruct((rows // CORES, width), BF16),
            in_specs=[anywhere] * len(args),
            out_specs=anywhere,
            scratch_shapes=scratch,
            compiler_params=pltpu.CompilerParams(
                collective_id=0, has_side_effects=True, vmem_limit_bytes=67_043_328),
        )(*args)

    return jax.shard_map(device_fn, mesh=mesh, in_specs=in_specs, out_specs=out_specs, check_vma=False)
```

time: 66 us -> 50 us (0.76)
  Pallas kernels: 64.4 us -> 48.4 us
    pallas_call x1, Pallas kernels: 64.4 us -> 48.4 us  [device_fn(): pl.pallas_call(functools.partial(layer_kernel, n_dev, n_side), out_shape=...]
where the time goes in v2:
time: 50 us; the launch traced here: 49.9 us
  Pallas kernels  48.4 us (97%)
  local copies, waits for them, and re-layouts  1.55 us (3%)
    pallas_call x1, Pallas kernels, device_fn(): pl.pallas_call(functools.partial(layer_kernel, n_dev, n_side), out_shape=...  48.4 us
    unnamed x1, local copies, waits for them, and re-layouts  1.55 us

profile of v2, /device:TPU:97, one launch (start us, length us, event | category | flops | bytes accessed | tf_op | source)
XLA Modules:
  0.0 49.9 jit_solution(10144619188919463524)
XLA Ops:
  0.0 48.4 %shard_map.127 = bf16[16,3584]{1,0:T(8,128)(2,1)} custom-call(bf16[128,3584]{1,0:T(8,128)(2,1)} %x_hbm.1, s32[1,128]{1,0:T(1,128)} %bitcast.17, f32[1,128]{1,0:T(1,128)} %constant.3.freq_hbm, bf16[128,8,64,256]{3,2,1,0:T(8,128)(2,1)} %bitcast.9, bf16[128,8,64,256]{3,2,1,0:T(8,128)(2,1)} %bitcast.10, bf16[56,64,4096]{2,1,0:T(8,128)(2,1)} %bitcast.11, ...), custom_call_target="tpu_custom_call" | custom-call | tf_op jit(solution)/shard_map/pallas_call | solution.py:491
  48.4 1.6 %copy.15 = bf16[16,3584]{1,0:T(8,128)(2,1)} copy(bf16[16,3584]{1,0:T(8,128)(2,1)} %shard_map.127) | data formatting | bytes 229376

commit v3 on v2

--- a/solution.py
+++ b/solution.py
@@ -57,7 +57,7 @@
                  x_hbm, len_hbm, freq_hbm, k_hbm, v_hbm, wq_hbm, wkv_hbm, wo_hbm, again_hbm, fgain_hbm,
                  wg_hbm, wu_hbm, wd_hbm, out_hbm,
                  act, lens, freqs, again, fgain, xres, wa, kbuf, vbuf, wo, wg, wu,
-                 yb, ub, qa, sb, pb, ob, osend, og, pp, precv, x1b, hg, u, r1, r2, r3, fin,
+                 yb, ub, lenc, osend, og, pp, precv, x1b, hg, u, r1, r2, r3, fin,
                  in_sem, w_sem, kv_sem, wo_sem, gu_sem, tail_sem, wd_sem, out_sem,
                  a2a_send, a2a_recv, pp_send, pp_recv, ag_send, ag_recv, u_send, u_recv,
                  rs_send, rs_recv, fin_send, fin_recv):
@@ -115,18 +115,28 @@
     def w_slot(j):
         return wa.at[:, :, j * COL:(j + 1) * COL]
 
-    load(wq_hbm.at[:, :, cols(side * q_cols, COL)], w_slot(0), w_sem.at[0], 0)
-    load(wq_hbm.at[:, :, cols(side * q_cols + COL, COL)], w_slot(1), w_sem.at[1], 0)
-    load(wkv_hbm.at[:, :, cols(side * head, COL)], w_slot(2), w_sem.at[2], 0)
-    load(wkv_hbm.at[:, :, cols(kv_half + side * head, COL)], w_slot(3), w_sem.at[3], 0)
+    load(wq_hbm.at[:, :, cols(side * q_cols, COL)], w_slot(0), w_sem.at[0])
+    load(wq_hbm.at[:, :, cols(side * q_cols + COL, COL)], w_slot(1), w_sem.at[1])
+    load(wkv_hbm.at[:, :, cols(side * head, COL)], w_slot(2), w_sem.at[2])
+    load(wkv_hbm.at[:, :, cols(kv_half + side * head, COL)], w_slot(3), w_sem.at[3])
     phase('wait_x')
     for i, ref in enumerate((act, lens, freqs, again, fgain, xres)):
         landed(ref, in_sem.at[i])
-    load(k_hbm.at[:, side], kbuf, kv_sem.at[0], 0)
-    load(v_hbm.at[:, side], vbuf, kv_sem.at[1], 0)
-    for r in range(n_x):
+    by_distance = sorted(range(1, n_x), key=lambda r: (-min(r, n_x - r), -r)) + [0]
+
+    def cache_rows(r):
+        return pl.ds(lax.rem(chip + r, n_x) * rows, rows)
+
+    def load_cache(r):
+        at = cache_rows(r)
+        load(k_hbm.at[at, side], kbuf.at[at], kv_sem.at[0, r])
+        load(v_hbm.at[at, side], vbuf.at[at], kv_sem.at[1, r])
+
+    def load_wo(r):
         src_chip = lax.rem(chip + n_x - r, n_x)
         load(wo_hbm.at[CORES * src_chip + core], wo.at[r], wo_sem.at[r])
+
+    load_cache(by_distance[0])
     phase('tables')
     row_id = lax.broadcasted_iota(jnp.int32, (seqs, seqs), 0)
     col_id = lax.broadcasted_iota(jnp.int32, (seqs, seqs), 1)
@@ -147,54 +157,83 @@
         act[:, part] = (act[:, part].astype(F32) * inv * again[:, part]).astype(BF16)
 
     phase('qkv')
-    @pl.loop(0, 4)
-    def _(j):
+    lenc[...] = len_col
+
+    for j in range(4):
         landed(w_slot(0), w_sem.at[j])
-        w = wa[:, :, cols(j * COL, COL)].reshape(prow * pcol, COL)
-        yb[j] = dot(act[...], w)
-
+        if j + 1 < n_x:
+            load_cache(by_distance[j + 1])
+        yb[j] = dot(act[...], wa[:, :, cols(j * COL, COL)].reshape(prow * pcol, COL))
+
+    load_wo(0)
+    load_wo(by_distance[1])
     phase('rope')
-    q0 = rotate(yb[0]).astype(BF16).astype(F32)
-    q1 = rotate(yb[1]).astype(BF16).astype(F32)
-    k_new = rotate(yb[2]).astype(BF16).astype(F32)
-    v_new = yb[3].astype(BF16).astype(F32)
-    qa[...] = pair_blocks(q0, q1).astype(BF16)
-    scale = head ** -0.5
-    self0 = jnp.sum(q0 * k_new, axis=1, keepdims=True)
-    self1 = jnp.sum(q1 * k_new, axis=1, keepdims=True)
-    self_score = pair_blocks(self0, self1) * scale
-    len_rows = pair_blocks(len_col, len_col).astype(jnp.int32)
+    for j in range(4):
+        vecs = yb[j] if j == 3 else rotate(yb[j])
+        yb[j] = vecs.astype(BF16).astype(F32)
 
     span = kbuf.shape[1]
     keys = 8 * span
-    phase('wait_k')
-    landed(kbuf, kv_sem.at[0])
-    phase('scores')
-    for b in range(seqs // 8):
-        k_blk = kbuf[8 * b:8 * b + 8].reshape(keys, head)
-        sb[16 * b:16 * b + 16, :] = lax.dot_general(
-            qa[16 * b:16 * b + 16, :], k_blk, (((1,), (1,)), ((), ())), preferred_element_type=F32)
-    phase('softmax')
-    row = lax.broadcasted_iota(jnp.int32, (2 * seqs, keys), 0)
-    key = lax.broadcasted_iota(jnp.int32, (2 * seqs, keys), 1)
+    scale = head ** -0.5
+    groups = rows // 8
+    row = lax.broadcasted_iota(jnp.int32, (2 * rows, keys), 0)
+    key = lax.broadcasted_iota(jnp.int32, (2 * rows, keys), 1)
     offset = key - lax.rem(row, 8) * span
-    valid = (offset >= 0) & (offset < len_rows)
-    scores = jnp.where(valid, sb[...] * scale, NEG)
-    row_max = jnp.maximum(jnp.max(scores, axis=1, keepdims=True), self_score)
-    exp_scores = jnp.exp(scores - row_max)
-    self_exp = jnp.exp(self_score - row_max)
-    total = jnp.sum(exp_scores, axis=1, keepdims=True) + self_exp
-    pb[...] = exp_scores.astype(BF16)
-    phase('wait_v')
-    landed(vbuf, kv_sem.at[1])
-    phase('mix')
-    for b in range(seqs // 8):
-        v_blk = vbuf[8 * b:8 * b + 8].reshape(keys, head)
-        ob[16 * b:16 * b + 16, :] = dot(pb[16 * b:16 * b + 16, :], v_blk)
-    mixed = ob[...] + self_exp.astype(BF16).astype(F32) * pair_blocks(v_new, v_new)
-    mixed = (mixed / total).reshape(seqs // 8, 16, head)
-    osend[:, :head] = mixed[:, :8].reshape(seqs, head).astype(BF16)
-    osend[:, head:] = mixed[:, 8:].reshape(seqs, head).astype(BF16)
+
+    def cat(parts):
+        return parts[0] if len(parts) == 1 else jnp.concatenate(parts, axis=0)
+
+    def attend(theres):
+        ats = [pl.ds(pl.multiple_of(there * rows, rows), rows) for there in theres]
+        q0, q1, k_new, v_new = (cat([yb[j, at, :] for at in ats]) for j in range(4))
+        q_pair = pair_blocks(q0, q1).astype(BF16)
+        self_score = pair_blocks(jnp.sum(q0 * k_new, axis=1, keepdims=True),
+                                 jnp.sum(q1 * k_new, axis=1, keepdims=True)) * scale
+        lengths = cat([lenc[at, :] for at in ats])
+        len_rows = pair_blocks(lengths, lengths).astype(jnp.int32)
+        blocks = [there * rows + 8 * b for there in theres for b in range(groups)]
+        scores = cat([
+            lax.dot_general(q_pair[16 * n:16 * n + 16], kbuf[pl.ds(b, 8)].reshape(keys, head),
+                            (((1,), (1,)), ((), ())), preferred_element_type=F32)
+            for n, b in enumerate(blocks)])
+        offsets = cat([offset] * len(theres))
+        scores = jnp.where((offsets >= 0) & (offsets < len_rows), scores * scale, NEG)
+        row_max = jnp.maximum(jnp.max(scores, axis=1, keepdims=True), self_score)
+        exp_scores = jnp.exp(scores - row_max)
+        self_exp = jnp.exp(self_score - row_max)
+        total = jnp.sum(exp_scores, axis=1, keepdims=True) + self_exp
+        probs = exp_scores.astype(BF16)
+        mixed = cat([dot(probs[16 * n:16 * n + 16], vbuf[pl.ds(b, 8)].reshape(keys, head))
+                     for n, b in enumerate(blocks)])
+        mixed = mixed + self_exp.astype(BF16).astype(F32) * pair_blocks(v_new, v_new)
+        mixed = (mixed / total).reshape(len(blocks), 16, head)
+        first = mixed[:, :8].reshape(len(theres) * rows, head).astype(BF16)
+        second = mixed[:, 8:].reshape(len(theres) * rows, head).astype(BF16)
+        for n, at in enumerate(ats):
+            osend[at, :head] = first[n * rows:(n + 1) * rows]
+            osend[at, head:] = second[n * rows:(n + 1) * rows]
+        return ats
+
+    def send(src, dst, send_sem, recv_sem, where):
+        pltpu.make_async_remote_copy(src, dst, send_sem, recv_sem, device_id=where, device_id_type=MESH).start()
+
+    def arrived(dst, sem):
+        pltpu.make_async_copy(dst, dst, sem).wait()
+
+    pl.semaphore_wait(barrier, len(peers))
+    for pair in (by_distance[:2], by_distance[2:]):
+        phase('wait_kv%d' % pair[0])
+        for r in pair:
+            landed(kbuf.at[cache_rows(r)], kv_sem.at[0, r])
+            landed(vbuf.at[cache_rows(r)], kv_sem.at[1, r])
+        phase('attend%d' % pair[0])
+        ats = attend([lax.rem(chip + r, n_x) for r in pair])
+        for r, at in zip(pair, ats):
+            if r:
+                send(osend.at[at], og.at[r], a2a_send.at[r], a2a_recv.at[r], on_x(r))
+        if pair[0] == by_distance[0]:
+            load_wo(by_distance[0])
+            load_wo(by_distance[2])
 
     phase('loads2')
     seg = ((0, kq), (half // pcol, kq), (kq, half // pcol - kq), (half // pcol + kq, half // pcol - kq))
@@ -211,22 +250,10 @@
 
     load_gate_up(0)
     load_gate_up(1)
-    phase('a2a_start')
-    pl.semaphore_wait(barrier, len(peers))
-
-    def send(src, dst, send_sem, recv_sem, where):
-        pltpu.make_async_remote_copy(src, dst, send_sem, recv_sem, device_id=where, device_id_type=MESH).start()
-
-    def arrived(dst, sem):
-        pltpu.make_async_copy(dst, dst, sem).wait()
-
-    for r in range(1, n_x):
-        there = lax.rem(chip + r, n_x)
-        send(osend.at[pl.ds(pl.multiple_of(there * rows, rows), rows)], og.at[r], a2a_send.at[r], a2a_recv.at[r], on_x(r))
-
     phase('proj')
-    steps = [0, 1] + [r for r in range(n_x - 1, 1, -1)]
+    steps = [0] + by_distance[1:-1] + by_distance[:1]
     for r in steps[:-1]:
+        phase('proj%d' % r)
         landed(wo.at[r], wo_sem.at[r])
         if r == 0:
             pp[...] = dot(osend[my_rows, :], wo[0])
@@ -234,6 +261,7 @@
             arrived(og.at[r], a2a_recv.at[r])
             pp[...] += dot(og[r], wo[r])
     r = steps[-1]
+    phase('proj%d' % r)
     landed(wo.at[r], wo_sem.at[r])
     arrived(og.at[r], a2a_recv.at[r])
     for i in range(2):
@@ -272,11 +300,17 @@
         arrived(piece(owner, strip, core), ag_recv.at[p, i])
 
     source = ((-1, 0), (1, 1), (-1, 1), (1, 0), (2, 0), (2, 1))
-    for p in range(2):
-        hop(dev, strips[p][0], p, 0, on_y(1))
-        hop(dev, strips[p][1], p, 1, on_y(-1))
-        hop(dev, strips[p][1], p, 2, on_y(1))
-        hop(dev, strips[p][0], p, 3, on_y(-1))
+    def hop_own(p, late):
+        if late:
+            hop(dev, strips[p][1], p, 2, on_y(1))
+            hop(dev, strips[p][0], p, 3, on_y(-1))
+        else:
+            hop(dev, strips[p][0], p, 0, on_y(1))
+            hop(dev, strips[p][1], p, 1, on_y(-1))
+
+    hop_own(0, False)
+    hop_own(0, True)
+    hop_own(1, False)
 
     def take(p, i):
         owner, strip = dev + source[i][0], strips[p][source[i][1]]
@@ -306,15 +340,20 @@
             out = term if out is None else out + term
         return out
 
-    def gate_up(p, j):
-        gate, up = partial_sum(0, j, p), partial_sum(1, j, p)
-        if p == 0:
-            yb[j] = gate
-            ub[j] = up
-        else:
-            here = u.at[core * n_col + j]
-            here[...] = (jax.nn.silu(yb[j] + gate) * (ub[j] + up)).astype(BF16)
-            send(here, here, u_send.at[j], u_recv.at[j], mate)
+    def gate_up(p, group):
+        for j in group:
+            gate, up = partial_sum(0, j, p), partial_sum(1, j, p)
+            if p == 0:
+                yb[j] = gate
+                ub[j] = up
+            else:
+                gate = yb[j] + gate
+                gate = 0.5 * gate * (1.0 + jnp.tanh(0.5 * gate))
+                u[:, cols(core * half + j * COL, COL)] = (gate * (ub[j] + up)).astype(BF16)
+        if p == 1:
+            for j in group:
+                here = u.at[:, cols(core * half + j * COL, COL)]
+                send(here, here, u_send.at[j], u_recv.at[j], mate)
 
     def gate_up_part(p):
         for i in (2 * p, 2 * p + 1):
@@ -325,94 +364,111 @@
                     landed(tail.at[pl.ds(t * prow + first, count)], tail_sem.at[m, t, i])
         phase('gateup%d' % p)
 
-        @pl.loop(0, n_main)
-        def _(j):
-            gate_up(p, j)
-
-        for t in range(n_tail):
-            gate_up(p, n_main + t)
-
-    for p, i in ((0, 0), (0, 1), (0, 2), (0, 3), (1, 0), (1, 1), (0, 4), (0, 5), (1, 2), (1, 3)):
+        if p == 0:
+            gate_up(p, range(n_col - 2))
+            phase('gather2')
+            for i in (2, 3, 4, 5):
+                take(1, i)
+            phase('gateup0b')
+            gate_up(p, range(n_col - 2, n_col))
+        else:
+            gate_up(p, range(3))
+            gate_up(p, range(3, 5))
+            gate_up(p, range(5, n_col))
+
+    take(0, 0)
+    take(0, 1)
+    hop_own(1, True)
+    phase('gather_b')
+    for p, i in ((0, 2), (0, 3), (1, 0), (1, 1)):
+        take(p, i)
+    phase('gather_c')
+    for p, i in ((0, 4), (0, 5)):
         take(p, i)
     from_mate(0)
     phase('wait_gu0')
     gate_up_part(0)
-    phase('gather2')
-    take(1, 4)
-    take(1, 5)
+    phase('gather3')
     from_mate(1)
     phase('wait_gu1')
     gate_up_part(1)
     phase('down0')
-    ahead = 3
+    ahead = 1
     fold_half = half // pcol
 
-    def u_half(whose):
-        return jnp.concatenate([u[whose * n_col + i] for i in range(n_col)], axis=1)
-
-    def down_half(whose, j):
+    def down_half(whose, group):
         at = pl.ds(whose * fold_half, fold_half)
-        return dot(u_half(whose), wa[at, :, cols(j * COL, COL)].reshape(half, COL))
-
-    @pl.loop(0, ahead)
-    def _(j):
-        landed(wa.at[:, :, 0:COL], wd_sem.at[j])
-        yb[j] = down_half(core, j)
+        part = slice(group[0] * COL, (group[-1] + 1) * COL)
+        return dot(u[:, cols(whose * half, half)], wa[at, :, part].reshape(half, len(group) * COL))
+
+    def keep(group, value, add):
+        for n, j in enumerate(group):
+            piece_of = value[:, n * COL:(n + 1) * COL]
+            yb[j] = yb[j] + piece_of if add else piece_of
+
+    pairs = [range(j, min(j + 2, n_col)) for j in range(0, n_col, 2)]
+    for group in pairs[:ahead]:
+        for j in group:
+            landed(wa.at[:, :, 0:COL], wd_sem.at[j])
+        keep(group, down_half(core, group), False)
 
     phase('wait_u')
     for j in range(n_col):
-        arrived(u.at[(1 - core) * n_col + j], u_recv.at[j])
+        arrived(u.at[:, cols((1 - core) * half + j * COL, COL)], u_recv.at[j])
 
     phase('down')
     def way(j):
-        sign = (1 - 2 * core) * (1 - 2 * lax.rem(j, 2))
+        sign = (1 - 2 * core) * (1 - 2 * (j % 2))
         return sign
 
     def rows_of(owner):
         return pl.ds(pl.multiple_of(lax.rem(owner + 2 * n_dev, n_dev) * rows, rows), rows)
 
-    def pass_on(j):
+    def pass_far(j):
+        send(yb.at[j, rows_of(dev + 2)], r1.at[j], rs_send.at[0, j], rs_recv.at[0, j], on_y(way(j)))
+
+    def pass_near(j):
         sign = way(j)
-        send(yb.at[j, rows_of(dev + 2)], r1.at[j], rs_send.at[0, j], rs_recv.at[0, j], on_y(sign))
         send(yb.at[j, rows_of(dev - sign)], r3.at[j], rs_send.at[2, j], rs_recv.at[2, j], on_y(-sign))
 
-    @pl.loop(0, ahead)
-    def _(j):
-        yb[j] += down_half(1 - core, j)
-        pass_on(j)
-
-    @pl.loop(ahead, n_col)
-    def _(j):
-        landed(wa.at[:, :, 0:COL], wd_sem.at[j])
-        yb[j] = dot(jnp.concatenate([u[i] for i in range(2 * n_col)], axis=1),
-                    wa[:, :, cols(j * COL, COL)].reshape(prow * pcol, COL))
-        pass_on(j)
-
-    phase('stage2')
-    @pl.loop(0, n_col)
-    def _(j):
+    def pass_sum(j):
         sign = way(j)
         arrived(r1.at[j], rs_recv.at[0, j])
         yb[j, rows_of(dev + sign), :] += r1[j]
         send(yb.at[j, rows_of(dev + sign)], r2.at[j], rs_send.at[1, j], rs_recv.at[1, j], on_y(sign))
 
+    for i, group in enumerate(pairs):
+        if i < ahead:
+            keep(group, down_half(1 - core, group), True)
+        else:
+            for j in group:
+                landed(wa.at[:, :, 0:COL], wd_sem.at[j])
+            part = slice(group[0] * COL, (group[-1] + 1) * COL)
+            keep(group, dot(u[...], wa[:, :, part].reshape(prow * pcol, len(group) * COL)), False)
+        for j in group:
+            pass_far(j)
+
+    phase('stage2')
+    for j in range(n_col):
+        pass_near(j)
+    for j in range(n_col):
+        pass_sum(j)
+
     phase('final')
-    @pl.loop(0, n_col)
-    def _(j):
+    blk = rows // CORES
+    my_blk = pl.ds(pl.multiple_of(core * blk, blk), blk)
+    mate_blk = pl.ds(pl.multiple_of((1 - core) * blk, blk), blk)
+    for j in range(n_col):
         arrived(r2.at[j], rs_recv.at[1, j])
         arrived(r3.at[j], rs_recv.at[2, j])
         y = (yb[j, rows_of(dev), :] + r2[j] + r3[j]).astype(BF16)
-        x1 = x1b[:, cols(core * half + j * COL, COL)]
-        fin[:, cols(j * COL, COL)] = (x1.astype(F32) + y.astype(F32)).astype(BF16)
-
+        here = cols(core * half + j * COL, COL)
+        fin[j] = (x1b[:, here].astype(F32) + y.astype(F32)).astype(BF16)
+        send(fin.at[j, mate_blk], out_hbm.at[:, here], fin_send.at[j], fin_recv.at[j], mate)
+        load(fin.at[j, my_blk], out_hbm.at[:, here], out_sem.at[j], 0)
     phase('fin')
-    blk = rows // CORES
-    my_blk = pl.ds(pl.multiple_of(core * blk, blk), blk)
-    mate_blk = pl.ds(pl.multiple_of((1 - core) * blk, blk), blk)
-    send(fin.at[mate_blk], out_hbm.at[:, mine], fin_send.at[0], fin_recv.at[0], mate)
-    store = pltpu.make_async_copy(fin.at[my_blk], out_hbm.at[:, mine], out_sem.at[0])
-    store.start()
-    arrived(out_hbm.at[:, other], fin_recv.at[0])
+    for j in range(n_col):
+        arrived(out_hbm.at[:, cols((1 - core) * half + j * COL, COL)], fin_recv.at[j])
     phase('drain')
     for r in range(1, n_x):
         arrived(og.at[r], a2a_send.at[r])
@@ -424,11 +480,12 @@
             strip = strips[p][(0, 1, 1, 0, 0, 1, 0, 1, 1, 0, 0, 1)[i]]
             arrived(piece(dev, strip, core), ag_send.at[p, i])
     for j in range(n_col):
-        arrived(u.at[0], u_send.at[j])
+        arrived(u.at[:, 0:COL], u_send.at[j])
         for i in range(3):
             arrived(r1.at[0], rs_send.at[i, j])
-    arrived(fin.at[mate_blk], fin_send.at[0])
-    store.wait()
+    for j in range(n_col):
+        arrived(fin.at[j, mate_blk], fin_send.at[j])
+        arrived(fin.at[j, my_blk], out_sem.at[j])
     phase(None)
 
 
@@ -476,16 +533,15 @@
             vmem((seqs, span, head), BF16), vmem((seqs, span, head), BF16),
             vmem((n_x, q_cols, width), BF16),
             vmem((tall, span, main), BF16), vmem((tall, span, main), BF16),
-            vmem((n_col, seqs, COL), F32), vmem((n_col, seqs, COL), F32), vmem((2 * seqs, head), BF16),
-            vmem((2 * seqs, 8 * span), F32), vmem((2 * seqs, 8 * span), BF16), vmem((2 * seqs, head), F32),
+            vmem((n_col, seqs, COL), F32), vmem((n_col, seqs, COL), F32), vmem((seqs, 1), F32),
             vmem((seqs, q_cols), BF16), vmem((n_x, rows, q_cols), BF16),
             vmem((rows, width), F32), vmem((rows, width), F32), vmem((rows, width), BF16),
-            vmem((n_dev * rows, width), BF16), vmem((2 * n_col, seqs, COL), BF16),
+            vmem((n_dev * rows, width), BF16), vmem((seqs, ff), BF16),
             vmem((n_col, rows, COL), F32), vmem((n_col, rows, COL), F32), vmem((n_col, rows, COL), F32),
-            vmem((rows, half), BF16),
-            dma((6,)), dma((4,)), dma((2,)), dma((n_x,)), dma((2, 4)), dma((2, 2, 4)), dma((n_col,)), dma((1,)),
+            vmem((n_col, rows, COL), BF16),
+            dma((6,)), dma((4,)), dma((2, n_x)), dma((n_x,)), dma((2, 4)), dma((2, 2, 4)), dma((n_col,)), dma((n_col,)),
             dma((n_x,)), dma((n_x,)), dma((2,)), dma((2,)), dma((2, 12)), dma((2, 12)), dma((n_col,)), dma((n_col,)),
-            dma((3, n_col)), dma((3, n_col)), dma((1,)), dma((1,)),
+            dma((3, n_col)), dma((3, n_col)), dma((n_col,)), dma((n_col,)),
         ]
         anywhere = pl.BlockSpec(memory_space=pl.ANY)
         return pl.pallas_call(

time: 50 us -> 47.7 us (0.954)
  Pallas kernels: 48.4 us -> 46 us
    pallas_call x1, Pallas kernels: 48.4 us -> 46 us  [device_fn(): pl.pallas_call(functools.partial(layer_kernel, n_dev, n_side), out_shape=...]
where the time goes in v3:
time: 47.7 us; the launch traced here: 47.6 us
  Pallas kernels  46 us (96%)
  local copies, waits for them, and re-layouts  1.55 us (3%)
    pallas_call x1, Pallas kernels, device_fn(): pl.pallas_call(functools.partial(layer_kernel, n_dev, n_side), out_shape=...  46 us
    unnamed x1, local copies, waits for them, and re-layouts  1.55 us

profile of v3, /device:TPU:97, one launch (start us, length us, event | category | flops | bytes accessed | tf_op | source)
XLA Modules:
  0.0 47.6 jit_solution(8551295156379948718)
XLA Ops:
  0.0 46.0 %shard_map.127 = bf16[16,3584]{1,0:T(8,128)(2,1)} custom-call(bf16[128,3584]{1,0:T(8,128)(2,1)} %x_hbm.1, s32[1,128]{1,0:T(1,128)} %bitcast.17, f32[1,128]{1,0:T(1,128)} %constant.3.freq_hbm, bf16[128,8,64,256]{3,2,1,0:T(8,128)(2,1)} %bitcast.9, bf16[128,8,64,256]{3,2,1,0:T(8,128)(2,1)} %bitcast.10, bf16[56,64,4096]{2,1,0:T(8,128)(2,1)} %bitcast.11, ...), custom_call_target="tpu_custom_call" | custom-call | tf_op jit(solution)/shard_map/pallas_call | solution.py:547
  46.0 1.6 %copy.15 = bf16[16,3584]{1,0:T(8,128)(2,1)} copy(bf16[16,3584]{1,0:T(8,128)(2,1)} %shard_map.127) | data formatting | bytes 229376

commit v4 on v3

--- a/solution.py
+++ b/solution.py
@@ -55,10 +55,10 @@
 
 def layer_kernel(n_dev, n_side,
                  x_hbm, len_hbm, freq_hbm, k_hbm, v_hbm, wq_hbm, wkv_hbm, wo_hbm, again_hbm, fgain_hbm,
-                 wg_hbm, wu_hbm, wd_hbm, out_hbm,
+                 wg_hbm, wu_hbm, wd_hbm, out,
                  act, lens, freqs, again, fgain, xres, wa, kbuf, vbuf, wo, wg, wu,
-                 yb, ub, lenc, osend, og, pp, precv, x1b, hg, u, r1, r2, r3, fin,
-                 in_sem, w_sem, kv_sem, wo_sem, gu_sem, tail_sem, wd_sem, out_sem,
+                 yb, ub, lenc, osend, og, pp, precv, x1b, hg, u, r1, r2, r3, r4,
+                 in_sem, w_sem, kv_sem, wo_sem, gu_sem, tail_sem, wd_sem,
                  a2a_send, a2a_recv, pp_send, pp_recv, ag_send, ag_recv, u_send, u_recv,
                  rs_send, rs_recv, fin_send, fin_recv):
     dev = lax.axis_index('dev')
@@ -73,14 +73,14 @@
     half = width // 2
     rows = xres.shape[0]
     n_col = half // COL
-    kq = (n_col + 1) // 2 * COL // wa.shape[1]
+    kq = n_col // 2 * COL // wa.shape[1]
     n_main = wg.shape[2] // COL
     n_tail = n_col - n_main
     kv_half = wkv_hbm.shape[2] // 2
     prow, pcol = wa.shape[0], wa.shape[1]
 
     def on_x(r):
-        return {'side': CORES * lax.rem(chip + r, n_x) + core}
+        return {'side': CORES * lax.rem(chip + r, n_x) + 1 - core}
 
     def on_y(r):
         return {'dev': lax.rem(dev + r + n_dev, n_dev)}
@@ -89,6 +89,7 @@
     phase('start')
     barrier = pltpu.get_barrier_semaphore()
     peers = [mate] + [on_x(r) for r in range(1, n_x)] + [on_y(1), on_y(-1)]
+    peers += [{**on_y(1), **mate}, {**on_y(-1), **mate}]
     for peer in peers:
         pl.semaphore_signal(barrier, inc=1, device_id=peer, device_id_type=MESH)
 
@@ -101,8 +102,8 @@
     def landed(dst, sem):
         pltpu.make_async_copy(dst, dst, sem).wait()
 
-    mine = cols(core * half, half)
-    other = cols((1 - core) * half, half)
+    cut = (n_col + 1) // 2 * 2 * COL
+    spans = (slice(0, cut), slice(cut, width))
     my_rows = pl.ds(pl.multiple_of(chip * rows, rows), rows)
 
     load(x_hbm, act, in_sem.at[0], 0)
@@ -132,9 +133,18 @@
         load(k_hbm.at[at, side], kbuf.at[at], kv_sem.at[0, r])
         load(v_hbm.at[at, side], vbuf.at[at], kv_sem.at[1, r])
 
+    order = [0] + by_distance[1:-1] + by_distance[:1]
+
+    def slot(r):
+        start = order.index(r) * q_cols
+        return slice(start, start + q_cols)
+
+    def wo_slot(r):
+        return wo.at[slot(r)]
+
     def load_wo(r):
-        src_chip = lax.rem(chip + n_x - r, n_x)
-        load(wo_hbm.at[CORES * src_chip + core], wo.at[r], wo_sem.at[r])
+        src_core = core if r == 0 else 1 - core
+        load(wo_hbm.at[CORES * lax.rem(chip + n_x - r, n_x) + src_core], wo_slot(r), wo_sem.at[r])
 
     load_cache(by_distance[0])
     phase('tables')
@@ -220,8 +230,11 @@
     def arrived(dst, sem):
         pltpu.make_async_copy(dst, dst, sem).wait()
 
+    def og_slot(r):
+        return og.at[:, slot(r)]
+
     pl.semaphore_wait(barrier, len(peers))
-    for pair in (by_distance[:2], by_distance[2:]):
+    for pair in (by_distance[:2], by_distance[2:3], by_distance[3:]):
         phase('wait_kv%d' % pair[0])
         for r in pair:
             landed(kbuf.at[cache_rows(r)], kv_sem.at[0, r])
@@ -230,7 +243,7 @@
         ats = attend([lax.rem(chip + r, n_x) for r in pair])
         for r, at in zip(pair, ats):
             if r:
-                send(osend.at[at], og.at[r], a2a_send.at[r], a2a_recv.at[r], on_x(r))
+                send(osend.at[at], og_slot(r), a2a_send.at[r], a2a_recv.at[r], on_x(r))
         if pair[0] == by_distance[0]:
             load_wo(by_distance[0])
             load_wo(by_distance[2])
@@ -251,30 +264,29 @@
     load_gate_up(0)
     load_gate_up(1)
     phase('proj')
-    steps = [0] + by_distance[1:-1] + by_distance[:1]
-    for r in steps[:-1]:
-        phase('proj%d' % r)
-        landed(wo.at[r], wo_sem.at[r])
-        if r == 0:
-            pp[...] = dot(osend[my_rows, :], wo[0])
-        else:
-            arrived(og.at[r], a2a_recv.at[r])
-            pp[...] += dot(og[r], wo[r])
-    r = steps[-1]
-    phase('proj%d' % r)
-    landed(wo.at[r], wo_sem.at[r])
-    arrived(og.at[r], a2a_recv.at[r])
-    for i in range(2):
-        part = slice(i * half, (i + 1) * half)
-        pp[:, part] += dot(og[r], wo[r, :, part])
+    phase('proj0')
+    landed(wo_slot(0), wo_sem.at[0])
+    pp[...] = dot(osend[my_rows, :], wo[0:q_cols, :])
+    def wait_heads(r):
+        landed(wo_slot(r), wo_sem.at[r])
+        arrived(og_slot(r), a2a_recv.at[r])
+
+    phase('proj1')
+    wait_heads(order[1])
+    pp[...] += dot(og[:, slot(order[1])], wo[slot(order[1]), :])
+    phase('wait_proj')
+    for r in order[2:]:
+        wait_heads(r)
+    phase('proj_rest')
+    for i, part in enumerate(spans):
+        pp[:, part] += dot(og[:, 2 * q_cols:], wo[2 * q_cols:, part])
         send(pp.at[:, part], precv.at[:, part], pp_send.at[i], pp_recv.at[i], mate)
     for j in range(n_col):
         load(wd_hbm.at[:, :, cols(core * half + j * COL, COL)], wa.at[:, :, j * COL:(j + 1) * COL], wd_sem.at[j])
 
     phase('wait_mate')
     dev_rows = pl.ds(pl.multiple_of(dev * rows, rows), rows)
-    for i in range(2):
-        part = slice(i * half, (i + 1) * half)
+    for i, part in enumerate(spans):
         arrived(precv.at[:, part], pp_recv.at[i])
         x1b[:, part] = (xres[:, part].astype(F32) + (pp[:, part] + precv[:, part])).astype(BF16)
     phase('norm2')
@@ -292,37 +304,44 @@
         owner_rows = pl.ds(pl.multiple_of(lax.rem(owner + 2 * n_dev, n_dev) * rows, rows), rows)
         return hg.at[owner_rows, cols(whose * half + strip[0], strip[1])]
 
-    def hop(owner, strip, p, i, where):
-        ref = piece(owner, strip, core)
+    def across(step):
+        return {**on_y(step), **mate}
+
+    def hop(owner, strip, p, i, where, whose):
+        ref = piece(owner, strip, whose)
         send(ref, ref, ag_send.at[p, i], ag_recv.at[p, i], where)
-
-    def came(owner, strip, p, i):
-        arrived(piece(owner, strip, core), ag_recv.at[p, i])
 
     source = ((-1, 0), (1, 1), (-1, 1), (1, 0), (2, 0), (2, 1))
     def hop_own(p, late):
         if late:
-            hop(dev, strips[p][1], p, 2, on_y(1))
-            hop(dev, strips[p][0], p, 3, on_y(-1))
+            hop(dev, strips[p][1], p, 2, across(1), core)
+            hop(dev, strips[p][0], p, 3, across(-1), core)
         else:
-            hop(dev, strips[p][0], p, 0, on_y(1))
-            hop(dev, strips[p][1], p, 1, on_y(-1))
+            hop(dev, strips[p][0], p, 0, across(1), core)
+            hop(dev, strips[p][1], p, 1, across(-1), core)
 
     hop_own(0, False)
     hop_own(0, True)
     hop_own(1, False)
 
+    def take_near(p, i):
+        owner = dev + 2 * i - 1
+        start = strips[p][0][0] + i * strips[p][0][1]
+        ref = piece(owner, (start, strips[p][0][1]), 1 - core)
+        arrived(ref, ag_recv.at[p, i])
+        send(ref, ref, ag_send.at[p, 4 + i], ag_recv.at[p, 4 + i], across(1 - 2 * i))
+        send(ref, ref, ag_send.at[p, 6 + i], ag_recv.at[p, 6 + i], mate)
+
     def take(p, i):
         owner, strip = dev + source[i][0], strips[p][source[i][1]]
-        came(owner, strip, p, i)
-        if i < 2:
-            hop(owner, strip, p, 4 + i, on_y(1 - 2 * i))
-        hop(owner, strip, p, 6 + i, mate)
+        whose = 1 - core if i < 4 else core
+        arrived(piece(owner, strip, whose), ag_recv.at[p, i])
+        hop(owner, strip, p, 6 + i, mate, whose)
 
     def from_mate(p):
         for i in range(6):
             owner, strip = dev + source[i][0], strips[p][source[i][1]]
-            arrived(piece(owner, strip, 1 - core), ag_recv.at[p, 6 + i])
+            arrived(piece(owner, strip, core if i < 4 else 1 - core), ag_recv.at[p, 6 + i])
 
     def weights(m, j, i):
         first, count = seg[i]
@@ -365,23 +384,26 @@
         phase('gateup%d' % p)
 
         if p == 0:
-            gate_up(p, range(n_col - 2))
+            gate_up(p, range(n_col - 4))
             phase('gather2')
             for i in (2, 3, 4, 5):
                 take(1, i)
             phase('gateup0b')
-            gate_up(p, range(n_col - 2, n_col))
+            gate_up(p, range(n_col - 4, n_col))
         else:
-            gate_up(p, range(3))
-            gate_up(p, range(3, 5))
-            gate_up(p, range(5, n_col))
-
-    take(0, 0)
-    take(0, 1)
+            gate_up(p, range(n_col - 3))
+            gate_up(p, range(n_col - 3, n_col - 1))
+            gate_up(p, range(n_col - 1, n_col))
+
+    near = 1 - jnp.minimum(dev, 1)
+    take_near(0, near)
+    take_near(0, 1 - near)
     hop_own(1, True)
     phase('gather_b')
-    for p, i in ((0, 2), (0, 3), (1, 0), (1, 1)):
-        take(p, i)
+    take(0, 2)
+    take(0, 3)
+    take_near(1, near)
+    take_near(1, 1 - near)
     phase('gather_c')
     for p, i in ((0, 4), (0, 5)):
         take(p, i)
@@ -393,7 +415,6 @@
     phase('wait_gu1')
     gate_up_part(1)
     phase('down0')
-    ahead = 1
     fold_half = half // pcol
 
     def down_half(whose, group):
@@ -407,9 +428,9 @@
             yb[j] = yb[j] + piece_of if add else piece_of
 
     pairs = [range(j, min(j + 2, n_col)) for j in range(0, n_col, 2)]
-    for group in pairs[:ahead]:
-        for j in group:
-            landed(wa.at[:, :, 0:COL], wd_sem.at[j])
+    for j in range(n_col):
+        landed(wa.at[:, :, 0:COL], wd_sem.at[j])
+    for group in pairs[:2]:
         keep(group, down_half(core, group), False)
 
     phase('wait_u')
@@ -424,25 +445,34 @@
     def rows_of(owner):
         return pl.ds(pl.multiple_of(lax.rem(owner + 2 * n_dev, n_dev) * rows, rows), rows)
 
+    blk = rows // CORES
+    sides = [{'side': CORES * chip + b} for b in range(CORES)]
+
+    def block_of(owner, b):
+        start = lax.rem(owner + 2 * n_dev, n_dev) * rows + b * blk
+        return pl.ds(pl.multiple_of(start, blk), blk)
+
     def pass_far(j):
-        send(yb.at[j, rows_of(dev + 2)], r1.at[j], rs_send.at[0, j], rs_recv.at[0, j], on_y(way(j)))
+        send(yb.at[j, rows_of(dev + 2)], r1.at[j], rs_send.at[0, 0, j], rs_recv.at[0, 0, j], on_y(way(j)))
 
     def pass_near(j):
         sign = way(j)
-        send(yb.at[j, rows_of(dev - sign)], r3.at[j], rs_send.at[2, j], rs_recv.at[2, j], on_y(-sign))
+        for b in range(CORES):
+            send(yb.at[j, block_of(dev - sign, b)], r3.at[core, j], rs_send.at[2, b, j], rs_recv.at[2, core, j],
+                 {**on_y(-sign), **sides[b]})
 
     def pass_sum(j):
         sign = way(j)
-        arrived(r1.at[j], rs_recv.at[0, j])
+        arrived(r1.at[j], rs_recv.at[0, 0, j])
         yb[j, rows_of(dev + sign), :] += r1[j]
-        send(yb.at[j, rows_of(dev + sign)], r2.at[j], rs_send.at[1, j], rs_recv.at[1, j], on_y(sign))
-
-    for i, group in enumerate(pairs):
-        if i < ahead:
+        for b in range(CORES):
+            send(yb.at[j, block_of(dev + sign, b)], r2.at[core, j], rs_send.at[1, b, j], rs_recv.at[1, core, j],
+                 {**on_y(sign), **sides[b]})
+
+    for group in pairs:
+        if group in pairs[:2]:
             keep(group, down_half(1 - core, group), True)
         else:
-            for j in group:
-                landed(wa.at[:, :, 0:COL], wd_sem.at[j])
             part = slice(group[0] * COL, (group[-1] + 1) * COL)
             keep(group, dot(u[...], wa[:, :, part].reshape(prow * pcol, len(group) * COL)), False)
         for j in group:
@@ -452,28 +482,28 @@
     for j in range(n_col):
         pass_near(j)
     for j in range(n_col):
+        send(yb.at[j, block_of(dev, 1 - core)], r4.at[j], fin_send.at[j], fin_recv.at[j], mate)
+    for j in range(n_col):
         pass_sum(j)
 
     phase('final')
-    blk = rows // CORES
     my_blk = pl.ds(pl.multiple_of(core * blk, blk), blk)
-    mate_blk = pl.ds(pl.multiple_of((1 - core) * blk, blk), blk)
-    for j in range(n_col):
-        arrived(r2.at[j], rs_recv.at[1, j])
-        arrived(r3.at[j], rs_recv.at[2, j])
-        y = (yb[j, rows_of(dev), :] + r2[j] + r3[j]).astype(BF16)
-        here = cols(core * half + j * COL, COL)
-        fin[j] = (x1b[:, here].astype(F32) + y.astype(F32)).astype(BF16)
-        send(fin.at[j, mate_blk], out_hbm.at[:, here], fin_send.at[j], fin_recv.at[j], mate)
-        load(fin.at[j, my_blk], out_hbm.at[:, here], out_sem.at[j], 0)
-    phase('fin')
-    for j in range(n_col):
-        arrived(out_hbm.at[:, cols((1 - core) * half + j * COL, COL)], fin_recv.at[j])
+
+    def finish(whose, j, own_sum):
+        arrived(r3.at[whose, j], rs_recv.at[2, whose, j])
+        arrived(r2.at[whose, j], rs_recv.at[1, whose, j])
+        y = (own_sum + r2[whose, j] + r3[whose, j]).astype(BF16)
+        here = cols(whose * half + j * COL, COL)
+        out[:, here] = (x1b[my_blk, here].astype(F32) + y.astype(F32)).astype(BF16)
+
+    for j in range(n_col):
+        arrived(r4.at[j], fin_recv.at[j])
+        finish(core, j, yb[j, block_of(dev, core), :])
+        finish(1 - core, j, r4[j])
     phase('drain')
     for r in range(1, n_x):
-        arrived(og.at[r], a2a_send.at[r])
-    for i in range(2):
-        part = slice(i * half, (i + 1) * half)
+        arrived(og_slot(r), a2a_send.at[r])
+    for i, part in enumerate(spans):
         arrived(precv.at[:, part], pp_send.at[i])
     for p in range(2):
         for i in range(12):
@@ -481,11 +511,12 @@
             arrived(piece(dev, strip, core), ag_send.at[p, i])
     for j in range(n_col):
         arrived(u.at[:, 0:COL], u_send.at[j])
-        for i in range(3):
-            arrived(r1.at[0], rs_send.at[i, j])
-    for j in range(n_col):
-        arrived(fin.at[j, mate_blk], fin_send.at[j])
-        arrived(fin.at[j, my_blk], out_sem.at[j])
+        arrived(r1.at[0], rs_send.at[0, 0, j])
+        for b in range(CORES):
+            arrived(r2.at[0, 0], rs_send.at[1, b, j])
+            arrived(r3.at[0, 0], rs_send.at[2, b, j])
+    for j in range(n_col):
+        arrived(r4.at[j], fin_send.at[j])
     phase(None)
 
 
@@ -531,24 +562,24 @@
             vmem((1, width), F32), vmem((1, width), F32), vmem((rows, width), BF16),
             vmem((tall, span, half), BF16),
             vmem((seqs, span, head), BF16), vmem((seqs, span, head), BF16),
-            vmem((n_x, q_cols, width), BF16),
+            vmem((n_x * q_cols, width), BF16),
             vmem((tall, span, main), BF16), vmem((tall, span, main), BF16),
             vmem((n_col, seqs, COL), F32), vmem((n_col, seqs, COL), F32), vmem((seqs, 1), F32),
-            vmem((seqs, q_cols), BF16), vmem((n_x, rows, q_cols), BF16),
+            vmem((seqs, q_cols), BF16), vmem((rows, n_x * q_cols), BF16),
             vmem((rows, width), F32), vmem((rows, width), F32), vmem((rows, width), BF16),
             vmem((n_dev * rows, width), BF16), vmem((seqs, ff), BF16),
-            vmem((n_col, rows, COL), F32), vmem((n_col, rows, COL), F32), vmem((n_col, rows, COL), F32),
-            vmem((n_col, rows, COL), BF16),
-            dma((6,)), dma((4,)), dma((2, n_x)), dma((n_x,)), dma((2, 4)), dma((2, 2, 4)), dma((n_col,)), dma((n_col,)),
+            vmem((n_col, rows, COL), F32), vmem((CORES, n_col, rows // CORES, COL), F32),
+            vmem((CORES, n_col, rows // CORES, COL), F32), vmem((n_col, rows // CORES, COL), F32),
+            dma((6,)), dma((4,)), dma((2, n_x)), dma((n_x,)), dma((2, 4)), dma((2, 2, 4)), dma((n_col,)),
             dma((n_x,)), dma((n_x,)), dma((2,)), dma((2,)), dma((2, 12)), dma((2, 12)), dma((n_col,)), dma((n_col,)),
-            dma((3, n_col)), dma((3, n_col)), dma((n_col,)), dma((n_col,)),
+            dma((3, CORES, n_col)), dma((3, CORES, n_col)), dma((n_col,)), dma((n_col,)),
         ]
         anywhere = pl.BlockSpec(memory_space=pl.ANY)
         return pl.pallas_call(
             functools.partial(layer_kernel, n_dev, n_side),
             out_shape=jax.ShapeDtypeStruct((rows // CORES, width), BF16),
             in_specs=[anywhere] * len(args),
-            out_specs=anywhere,
+            out_specs=pl.BlockSpec(memory_space=pltpu.VMEM),
             scratch_shapes=scratch,
             compiler_params=pltpu.CompilerParams(
                 collective_id=0, has_side_effects=True, vmem_limit_bytes=67_043_328),

time: 47.7 us -> 45.3 us (0.950)
  Pallas kernels: 46 us -> 43.6 us
    pallas_call x1, Pallas kernels: 46 us -> 43.6 us  [device_fn(): pl.pallas_call(functools.partial(layer_kernel, n_dev, n_side), out_shape=...]
where the time goes in v4:
time: 45.3 us; the launch traced here: 45.2 us
  Pallas kernels  43.6 us (96%)
  local copies, waits for them, and re-layouts  1.55 us (3%)
    pallas_call x1, Pallas kernels, device_fn(): pl.pallas_call(functools.partial(layer_kernel, n_dev, n_side), out_shape=...  43.6 us
    unnamed x1, local copies, waits for them, and re-layouts  1.55 us

profile of v4, /device:TPU:97, one launch (start us, length us, event | category | flops | bytes accessed | tf_op | source)
XLA Modules:
  0.0 45.2 jit_solution(12493236579474602577)
XLA Ops:
  0.0 43.6 %shard_map.127 = bf16[16,3584]{1,0:T(8,128)(2,1)} custom-call(bf16[128,3584]{1,0:T(8,128)(2,1)} %x_hbm.1, s32[1,128]{1,0:T(1,128)} %bitcast.17, f32[1,128]{1,0:T(1,128)} %constant.3.freq_hbm, bf16[128,8,64,256]{3,2,1,0:T(8,128)(2,1)} %bitcast.9, bf16[128,8,64,256]{3,2,1,0:T(8,128)(2,1)} %bitcast.10, bf16[56,64,4096]{2,1,0:T(8,128)(2,1)} %bitcast.11, ...), custom_call_target="tpu_custom_call" | custom-call | tf_op jit(solution)/shard_map/pallas_call | solution.py:578
  43.6 1.6 %copy.15 = bf16[16,3584]{1,0:T(8,128)(2,1)} copy(bf16[16,3584]{1,0:T(8,128)(2,1)} %shard_map.127) | data formatting | bytes 229376

commit v5 on v4

--- a/solution.py
+++ b/solution.py
@@ -60,7 +60,7 @@
                  yb, ub, lenc, osend, og, pp, precv, x1b, hg, u, r1, r2, r3, r4,
                  in_sem, w_sem, kv_sem, wo_sem, gu_sem, tail_sem, wd_sem,
                  a2a_send, a2a_recv, pp_send, pp_recv, ag_send, ag_recv, u_send, u_recv,
-                 rs_send, rs_recv, fin_send, fin_recv):
+                 rs_send, rs_recv, far_recv, fin_send, fin_recv):
     dev = lax.axis_index('dev')
     side = lax.axis_index('side')
     n_x = n_side // CORES
@@ -130,8 +130,9 @@
 
     def load_cache(r):
         at = cache_rows(r)
-        load(k_hbm.at[at, side], kbuf.at[at], kv_sem.at[0, r])
-        load(v_hbm.at[at, side], vbuf.at[at], kv_sem.at[1, r])
+        group = max(by_distance.index(r) - 1, 0)
+        load(k_hbm.at[at, side], kbuf.at[at], kv_sem.at[group])
+        load(v_hbm.at[at, side], vbuf.at[at], kv_sem.at[group])
 
     order = [0] + by_distance[1:-1] + by_distance[:1]
 
@@ -144,9 +145,10 @@
 
     def load_wo(r):
         src_core = core if r == 0 else 1 - core
-        load(wo_hbm.at[CORES * lax.rem(chip + n_x - r, n_x) + src_core], wo_slot(r), wo_sem.at[r])
+        load(wo_hbm.at[CORES * lax.rem(chip + n_x - r, n_x) + src_core], wo_slot(r), wo_sem.at[min(order.index(r), 2)])
 
     load_cache(by_distance[0])
+    load_cache(by_distance[1])
     phase('tables')
     row_id = lax.broadcasted_iota(jnp.int32, (seqs, seqs), 0)
     col_id = lax.broadcasted_iota(jnp.int32, (seqs, seqs), 1)
@@ -171,10 +173,11 @@
 
     for j in range(4):
         landed(w_slot(0), w_sem.at[j])
-        if j + 1 < n_x:
-            load_cache(by_distance[j + 1])
+        if j == 3:
+            load_cache(by_distance[2])
         yb[j] = dot(act[...], wa[:, :, cols(j * COL, COL)].reshape(prow * pcol, COL))
 
+    load_cache(by_distance[3])
     load_wo(0)
     load_wo(by_distance[1])
     phase('rope')
@@ -234,16 +237,14 @@
         return og.at[:, slot(r)]
 
     pl.semaphore_wait(barrier, len(peers))
-    for pair in (by_distance[:2], by_distance[2:3], by_distance[3:]):
+    for group, pair in enumerate((by_distance[:2], by_distance[2:3], by_distance[3:])):
         phase('wait_kv%d' % pair[0])
-        for r in pair:
-            landed(kbuf.at[cache_rows(r)], kv_sem.at[0, r])
-            landed(vbuf.at[cache_rows(r)], kv_sem.at[1, r])
+        landed(kbuf.at[pl.ds(0, 2 * len(pair) * rows)], kv_sem.at[group])
         phase('attend%d' % pair[0])
         ats = attend([lax.rem(chip + r, n_x) for r in pair])
         for r, at in zip(pair, ats):
             if r:
-                send(osend.at[at], og_slot(r), a2a_send.at[r], a2a_recv.at[r], on_x(r))
+                send(osend.at[at], og_slot(r), a2a_send.at[0], a2a_recv.at[min(order.index(r), 2)], on_x(r))
         if pair[0] == by_distance[0]:
             load_wo(by_distance[0])
             load_wo(by_distance[2])
@@ -256,33 +257,34 @@
             first, count = seg[i]
             at = pl.ds(first, count)
             for m, (w_hbm, w_buf, tail) in enumerate(((wg_hbm, wg, kbuf), (wu_hbm, wu, vbuf))):
-                load(w_hbm.at[at, :, cols(core * half, n_main * COL)], w_buf.at[at], gu_sem.at[m, i])
+                load(w_hbm.at[at, :, cols(core * half, n_main * COL)], w_buf.at[at], gu_sem.at[m, part])
                 for t in range(n_tail):
                     load(w_hbm.at[at, :, cols(core * half + (n_main + t) * COL, COL)],
-                         tail.at[pl.ds(t * prow + first, count)], tail_sem.at[m, t, i])
+                         tail.at[pl.ds(t * prow + first, count)], tail_sem.at[m, part])
 
     load_gate_up(0)
     load_gate_up(1)
     phase('proj')
+    def tall_dot(lhs, rhs):
+        return dot(jnp.concatenate([lhs] * 4, axis=0), rhs)[:rows]
+
     phase('proj0')
     landed(wo_slot(0), wo_sem.at[0])
     pp[...] = dot(osend[my_rows, :], wo[0:q_cols, :])
-    def wait_heads(r):
-        landed(wo_slot(r), wo_sem.at[r])
-        arrived(og_slot(r), a2a_recv.at[r])
-
+    rest = slice(2 * q_cols, n_x * q_cols)
     phase('proj1')
-    wait_heads(order[1])
-    pp[...] += dot(og[:, slot(order[1])], wo[slot(order[1]), :])
+    landed(wo_slot(order[1]), wo_sem.at[1])
+    arrived(og_slot(order[1]), a2a_recv.at[1])
+    pp[...] += tall_dot(og[:, slot(order[1])], wo[slot(order[1]), :])
     phase('wait_proj')
-    for r in order[2:]:
-        wait_heads(r)
+    landed(wo.at[rest], wo_sem.at[2])
+    arrived(og.at[:, rest], a2a_recv.at[2])
     phase('proj_rest')
     for i, part in enumerate(spans):
-        pp[:, part] += dot(og[:, 2 * q_cols:], wo[2 * q_cols:, part])
-        send(pp.at[:, part], precv.at[:, part], pp_send.at[i], pp_recv.at[i], mate)
+        pp[:, part] += tall_dot(og[:, 2 * q_cols:], wo[2 * q_cols:, part])
+        send(pp.at[:, part], precv.at[:, part], pp_send.at[0], pp_recv.at[i], mate)
     for j in range(n_col):
-        load(wd_hbm.at[:, :, cols(core * half + j * COL, COL)], wa.at[:, :, j * COL:(j + 1) * COL], wd_sem.at[j])
+        load(wd_hbm.at[:, :, cols(core * half + j * COL, COL)], wa.at[:, :, j * COL:(j + 1) * COL], wd_sem.at[0])
 
     phase('wait_mate')
     dev_rows = pl.ds(pl.multiple_of(dev * rows, rows), rows)
@@ -307,9 +309,11 @@
     def across(step):
         return {**on_y(step), **mate}
 
+    kind = (0, 1, 2, 2, 3, 3) + (4,) * 6
+
     def hop(owner, strip, p, i, where, whose):
         ref = piece(owner, strip, whose)
-        send(ref, ref, ag_send.at[p, i], ag_recv.at[p, i], where)
+        send(ref, ref, ag_send.at[0], ag_recv.at[p, kind[i]], where)
 
     source = ((-1, 0), (1, 1), (-1, 1), (1, 0), (2, 0), (2, 1))
     def hop_own(p, late):
@@ -329,19 +333,20 @@
         start = strips[p][0][0] + i * strips[p][0][1]
         ref = piece(owner, (start, strips[p][0][1]), 1 - core)
         arrived(ref, ag_recv.at[p, i])
-        send(ref, ref, ag_send.at[p, 4 + i], ag_recv.at[p, 4 + i], across(1 - 2 * i))
-        send(ref, ref, ag_send.at[p, 6 + i], ag_recv.at[p, 6 + i], mate)
-
-    def take(p, i):
-        owner, strip = dev + source[i][0], strips[p][source[i][1]]
-        whose = 1 - core if i < 4 else core
-        arrived(piece(owner, strip, whose), ag_recv.at[p, i])
-        hop(owner, strip, p, 6 + i, mate, whose)
+        send(ref, ref, ag_send.at[0], ag_recv.at[p, 3], across(1 - 2 * i))
+        send(ref, ref, ag_send.at[0], ag_recv.at[p, 4], mate)
+
+    def both(p, count):
+        return hg.at[0:rows, 0:count * strips[p][0][1]]
+
+    def take_pair(p, first):
+        arrived(both(p, 2), ag_recv.at[p, kind[first]])
+        for i in (first, first + 1):
+            owner, strip = dev + source[i][0], strips[p][source[i][1]]
+            hop(owner, strip, p, 6 + i, mate, 1 - core if i < 4 else core)
 
     def from_mate(p):
-        for i in range(6):
-            owner, strip = dev + source[i][0], strips[p][source[i][1]]
-            arrived(piece(owner, strip, core if i < 4 else 1 - core), ag_recv.at[p, 6 + i])
+        arrived(both(p, 6), ag_recv.at[p, 4])
 
     def weights(m, j, i):
         first, count = seg[i]
@@ -372,22 +377,20 @@
         if p == 1:
             for j in group:
                 here = u.at[:, cols(core * half + j * COL, COL)]
-                send(here, here, u_send.at[j], u_recv.at[j], mate)
+                send(here, here, u_send.at[0], u_recv.at[0], mate)
 
     def gate_up_part(p):
-        for i in (2 * p, 2 * p + 1):
-            first, count = seg[i]
-            for m, (w_buf, tail) in enumerate(((wg, kbuf), (wu, vbuf))):
-                landed(w_buf.at[pl.ds(first, count)], gu_sem.at[m, i])
-                for t in range(n_tail):
-                    landed(tail.at[pl.ds(t * prow + first, count)], tail_sem.at[m, t, i])
+        count = seg[2 * p][1]
+        for m, (w_buf, tail) in enumerate(((wg, kbuf), (wu, vbuf))):
+            landed(w_buf.at[pl.ds(0, 2 * count)], gu_sem.at[m, p])
+            landed(tail.at[pl.ds(0, 2 * n_tail * count)], tail_sem.at[m, p])
         phase('gateup%d' % p)
 
         if p == 0:
             gate_up(p, range(n_col - 4))
             phase('gather2')
-            for i in (2, 3, 4, 5):
-                take(1, i)
+            take_pair(1, 2)
+            take_pair(1, 4)
             phase('gateup0b')
             gate_up(p, range(n_col - 4, n_col))
         else:
@@ -400,13 +403,11 @@
     take_near(0, 1 - near)
     hop_own(1, True)
     phase('gather_b')
-    take(0, 2)
-    take(0, 3)
+    take_pair(0, 2)
     take_near(1, near)
     take_near(1, 1 - near)
     phase('gather_c')
-    for p, i in ((0, 4), (0, 5)):
-        take(p, i)
+    take_pair(0, 4)
     from_mate(0)
     phase('wait_gu0')
     gate_up_part(0)
@@ -428,14 +429,12 @@
             yb[j] = yb[j] + piece_of if add else piece_of
 
     pairs = [range(j, min(j + 2, n_col)) for j in range(0, n_col, 2)]
-    for j in range(n_col):
-        landed(wa.at[:, :, 0:COL], wd_sem.at[j])
+    landed(wa, wd_sem.at[0])
     for group in pairs[:2]:
         keep(group, down_half(core, group), False)
 
     phase('wait_u')
-    for j in range(n_col):
-        arrived(u.at[:, cols((1 - core) * half + j * COL, COL)], u_recv.at[j])
+    arrived(u.at[:, cols((1 - core) * half, half)], u_recv.at[0])
 
     phase('down')
     def way(j):
@@ -453,20 +452,20 @@
         return pl.ds(pl.multiple_of(start, blk), blk)
 
     def pass_far(j):
-        send(yb.at[j, rows_of(dev + 2)], r1.at[j], rs_send.at[0, 0, j], rs_recv.at[0, 0, j], on_y(way(j)))
+        send(yb.at[j, rows_of(dev + 2)], r1.at[j], rs_send.at[0], far_recv.at[j], on_y(way(j)))
 
     def pass_near(j):
         sign = way(j)
         for b in range(CORES):
-            send(yb.at[j, block_of(dev - sign, b)], r3.at[core, j], rs_send.at[2, b, j], rs_recv.at[2, core, j],
+            send(yb.at[j, block_of(dev - sign, b)], r3.at[core, j], rs_send.at[2], rs_recv.at[1],
                  {**on_y(-sign), **sides[b]})
 
     def pass_sum(j):
         sign = way(j)
-        arrived(r1.at[j], rs_recv.at[0, 0, j])
+        arrived(r1.at[j], far_recv.at[j])
         yb[j, rows_of(dev + sign), :] += r1[j]
         for b in range(CORES):
-            send(yb.at[j, block_of(dev + sign, b)], r2.at[core, j], rs_send.at[1, b, j], rs_recv.at[1, core, j],
+            send(yb.at[j, block_of(dev + sign, b)], r2.at[core, j], rs_send.at[1], rs_recv.at[0],
                  {**on_y(sign), **sides[b]})
 
     for group in pairs:
@@ -482,7 +481,7 @@
     for j in range(n_col):
         pass_near(j)
     for j in range(n_col):
-        send(yb.at[j, block_of(dev, 1 - core)], r4.at[j], fin_send.at[j], fin_recv.at[j], mate)
+        send(yb.at[j, block_of(dev, 1 - core)], r4.at[j], fin_send.at[0], fin_recv.at[0], mate)
     for j in range(n_col):
         pass_sum(j)
 
@@ -490,33 +489,25 @@
     my_blk = pl.ds(pl.multiple_of(core * blk, blk), blk)
 
     def finish(whose, j, own_sum):
-        arrived(r3.at[whose, j], rs_recv.at[2, whose, j])
-        arrived(r2.at[whose, j], rs_recv.at[1, whose, j])
         y = (own_sum + r2[whose, j] + r3[whose, j]).astype(BF16)
         here = cols(whose * half + j * COL, COL)
         out[:, here] = (x1b[my_blk, here].astype(F32) + y.astype(F32)).astype(BF16)
 
+    arrived(r4, fin_recv.at[0])
+    arrived(r3, rs_recv.at[1])
+    arrived(r2, rs_recv.at[0])
     for j in range(n_col):
-        arrived(r4.at[j], fin_recv.at[j])
         finish(core, j, yb[j, block_of(dev, core), :])
         finish(1 - core, j, r4[j])
     phase('drain')
-    for r in range(1, n_x):
-        arrived(og_slot(r), a2a_send.at[r])
-    for i, part in enumerate(spans):
-        arrived(precv.at[:, part], pp_send.at[i])
-    for p in range(2):
-        for i in range(12):
-            strip = strips[p][(0, 1, 1, 0, 0, 1, 0, 1, 1, 0, 0, 1)[i]]
-            arrived(piece(dev, strip, core), ag_send.at[p, i])
-    for j in range(n_col):
-        arrived(u.at[:, 0:COL], u_send.at[j])
-        arrived(r1.at[0], rs_send.at[0, 0, j])
-        for b in range(CORES):
-            arrived(r2.at[0, 0], rs_send.at[1, b, j])
-            arrived(r3.at[0, 0], rs_send.at[2, b, j])
-    for j in range(n_col):
-        arrived(r4.at[j], fin_send.at[j])
+    arrived(og.at[:, q_cols:], a2a_send.at[0])
+    arrived(pp, pp_send.at[0])
+    arrived(hg.at[0:(CORES + 1) * rows], ag_send.at[0])
+    arrived(u.at[:, cols(core * half, half)], u_send.at[0])
+    arrived(r1, rs_send.at[0])
+    arrived(r2, rs_send.at[1])
+    arrived(r3, rs_send.at[2])
+    arrived(r4, fin_send.at[0])
     phase(None)
 
 
@@ -570,9 +561,9 @@
             vmem((n_dev * rows, width), BF16), vmem((seqs, ff), BF16),
             vmem((n_col, rows, COL), F32), vmem((CORES, n_col, rows // CORES, COL), F32),
             vmem((CORES, n_col, rows // CORES, COL), F32), vmem((n_col, rows // CORES, COL), F32),
-            dma((6,)), dma((4,)), dma((2, n_x)), dma((n_x,)), dma((2, 4)), dma((2, 2, 4)), dma((n_col,)),
-            dma((n_x,)), dma((n_x,)), dma((2,)), dma((2,)), dma((2, 12)), dma((2, 12)), dma((n_col,)), dma((n_col,)),
-            dma((3, CORES, n_col)), dma((3, CORES, n_col)), dma((n_col,)), dma((n_col,)),
+            dma((6,)), dma((4,)), dma((3,)), dma((3,)), dma((2, 2)), dma((2, 2)), dma((1,)),
+            dma((1,)), dma((3,)), dma((1,)), dma((2,)), dma((1,)), dma((2, 5)), dma((1,)), dma((1,)),
+            dma((3,)), dma((2,)), dma((n_col,)), dma((1,)), dma((1,)),
         ]
         anywhere = pl.BlockSpec(memory_space=pl.ANY)
         return pl.pallas_call(

time: 45.3 us -> 43.6 us (0.962)
  Pallas kernels: 43.6 us -> 41.9 us
    pallas_call x1, Pallas kernels: 43.6 us -> 41.9 us  [device_fn(): pl.pallas_call(functools.partial(layer_kernel, n_dev, n_side), out_shape=...]
where the time goes in v5:
time: 43.6 us; the launch traced here: 43.5 us
  Pallas kernels  41.9 us (96%)
  local copies, waits for them, and re-layouts  1.55 us (4%)
    pallas_call x1, Pallas kernels, device_fn(): pl.pallas_call(functools.partial(layer_kernel, n_dev, n_side), out_shape=...  41.9 us
    unnamed x1, local copies, waits for them, and re-layouts  1.55 us

profile of v5, /device:TPU:97, one launch (start us, length us, event | category | flops | bytes accessed | tf_op | source)
XLA Modules:
  0.0 43.5 jit_solution(13914332442260047889)
XLA Ops:
  0.0 41.9 %shard_map.127 = bf16[16,3584]{1,0:T(8,128)(2,1)} custom-call(bf16[128,3584]{1,0:T(8,128)(2,1)} %x_hbm.1, s32[1,128]{1,0:T(1,128)} %bitcast.17, f32[1,128]{1,0:T(1,128)} %constant.3.freq_hbm, bf16[128,8,64,256]{3,2,1,0:T(8,128)(2,1)} %bitcast.9, bf16[128,8,64,256]{3,2,1,0:T(8,128)(2,1)} %bitcast.10, bf16[56,64,4096]{2,1,0:T(8,128)(2,1)} %bitcast.11, ...), custom_call_target="tpu_custom_call" | custom-call | tf_op jit(solution)/shard_map/pallas_call | solution.py:569
  41.9 1.6 %copy.15 = bf16[16,3584]{1,0:T(8,128)(2,1)} copy(bf16[16,3584]{1,0:T(8,128)(2,1)} %shard_map.127) | data formatting | bytes 229376

commit v6 on v5

--- a/solution.py
+++ b/solution.py
@@ -73,7 +73,7 @@
     half = width // 2
     rows = xres.shape[0]
     n_col = half // COL
-    kq = n_col // 2 * COL // wa.shape[1]
+    kq = (n_col + 1) // 2 * COL // wa.shape[1]
     n_main = wg.shape[2] // COL
     n_tail = n_col - n_main
     kv_half = wkv_hbm.shape[2] // 2
@@ -123,18 +123,18 @@
     phase('wait_x')
     for i, ref in enumerate((act, lens, freqs, again, fgain, xres)):
         landed(ref, in_sem.at[i])
-    by_distance = sorted(range(1, n_x), key=lambda r: (-min(r, n_x - r), -r)) + [0]
+    by_distance = sorted(range(1, n_x), key=lambda r: (-min(r, n_x - r), r)) + [0]
 
     def cache_rows(r):
         return pl.ds(lax.rem(chip + r, n_x) * rows, rows)
 
     def load_cache(r):
         at = cache_rows(r)
-        group = max(by_distance.index(r) - 1, 0)
+        group = by_distance.index(r)
         load(k_hbm.at[at, side], kbuf.at[at], kv_sem.at[group])
         load(v_hbm.at[at, side], vbuf.at[at], kv_sem.at[group])
 
-    order = [0] + by_distance[1:-1] + by_distance[:1]
+    order = [0] + by_distance[:-1]
 
     def slot(r):
         start = order.index(r) * q_cols
@@ -148,7 +148,6 @@
         load(wo_hbm.at[CORES * lax.rem(chip + n_x - r, n_x) + src_core], wo_slot(r), wo_sem.at[min(order.index(r), 2)])
 
     load_cache(by_distance[0])
-    load_cache(by_distance[1])
     phase('tables')
     row_id = lax.broadcasted_iota(jnp.int32, (seqs, seqs), 0)
     col_id = lax.broadcasted_iota(jnp.int32, (seqs, seqs), 1)
@@ -173,13 +172,12 @@
 
     for j in range(4):
         landed(w_slot(0), w_sem.at[j])
-        if j == 3:
-            load_cache(by_distance[2])
+        if j:
+            load_cache(by_distance[j])
         yb[j] = dot(act[...], wa[:, :, cols(j * COL, COL)].reshape(prow * pcol, COL))
 
-    load_cache(by_distance[3])
     load_wo(0)
-    load_wo(by_distance[1])
+    load_wo(order[1])
     phase('rope')
     for j in range(4):
         vecs = yb[j] if j == 3 else rotate(yb[j])
@@ -237,7 +235,7 @@
         return og.at[:, slot(r)]
 
     pl.semaphore_wait(barrier, len(peers))
-    for group, pair in enumerate((by_distance[:2], by_distance[2:3], by_distance[3:])):
+    for group, pair in enumerate([[r] for r in by_distance]):
         phase('wait_kv%d' % pair[0])
         landed(kbuf.at[pl.ds(0, 2 * len(pair) * rows)], kv_sem.at[group])
         phase('attend%d' % pair[0])
@@ -246,8 +244,8 @@
             if r:
                 send(osend.at[at], og_slot(r), a2a_send.at[0], a2a_recv.at[min(order.index(r), 2)], on_x(r))
         if pair[0] == by_distance[0]:
-            load_wo(by_distance[0])
-            load_wo(by_distance[2])
+            for other in order[2:]:
+                load_wo(other)
 
     phase('loads2')
     seg = ((0, kq), (half // pcol, kq), (kq, half // pcol - kq), (half // pcol + kq, half // pcol - kq))
@@ -394,9 +392,8 @@
             phase('gateup0b')
             gate_up(p, range(n_col - 4, n_col))
         else:
-            gate_up(p, range(n_col - 3))
-            gate_up(p, range(n_col - 3, n_col - 1))
-            gate_up(p, range(n_col - 1, n_col))
+            gate_up(p, range(n_col - 2))
+            gate_up(p, range(n_col - 2, n_col))
 
     near = 1 - jnp.minimum(dev, 1)
     take_near(0, near)
@@ -561,7 +558,7 @@
             vmem((n_dev * rows, width), BF16), vmem((seqs, ff), BF16),
             vmem((n_col, rows, COL), F32), vmem((CORES, n_col, rows // CORES, COL), F32),
             vmem((CORES, n_col, rows // CORES, COL), F32), vmem((n_col, rows // CORES, COL), F32),
-            dma((6,)), dma((4,)), dma((3,)), dma((3,)), dma((2, 2)), dma((2, 2)), dma((1,)),
+            dma((6,)), dma((4,)), dma((n_x,)), dma((3,)), dma((2, 2)), dma((2, 2)), dma((1,)),
             dma((1,)), dma((3,)), dma((1,)), dma((2,)), dma((1,)), dma((2, 5)), dma((1,)), dma((1,)),
             dma((3,)), dma((2,)), dma((n_col,)), dma((1,)), dma((1,)),
         ]

time: 43.6 us -> 42.3 us (0.970)
  Pallas kernels: 41.9 us -> 40.6 us
    pallas_call x1, Pallas kernels: 41.9 us -> 40.6 us  [device_fn(): pl.pallas_call(functools.partial(layer_kernel, n_dev, n_side), out_shape=...]
where the time goes in v6:
time: 42.3 us; the launch traced here: 42.2 us
  Pallas kernels  40.6 us (96%)
  local copies, waits for them, and re-layouts  1.55 us (4%)
    pallas_call x1, Pallas kernels, device_fn(): pl.pallas_call(functools.partial(layer_kernel, n_dev, n_side), out_shape=...  40.6 us
    unnamed x1, local copies, waits for them, and re-layouts  1.55 us

profile of v6, /device:TPU:97, one launch (start us, length us, event | category | flops | bytes accessed | tf_op | source)
XLA Modules:
  0.0 42.2 jit_solution(1747165511485297809)
XLA Ops:
  0.0 40.6 %shard_map.127 = bf16[16,3584]{1,0:T(8,128)(2,1)} custom-call(bf16[128,3584]{1,0:T(8,128)(2,1)} %x_hbm.1, s32[1,128]{1,0:T(1,128)} %bitcast.17, f32[1,128]{1,0:T(1,128)} %constant.3.freq_hbm, bf16[128,8,64,256]{3,2,1,0:T(8,128)(2,1)} %bitcast.9, bf16[128,8,64,256]{3,2,1,0:T(8,128)(2,1)} %bitcast.10, bf16[56,64,4096]{2,1,0:T(8,128)(2,1)} %bitcast.11, ...), custom_call_target="tpu_custom_call" | custom-call | tf_op jit(solution)/shard_map/pallas_call | solution.py:566
  40.6 1.6 %copy.15 = bf16[16,3584]{1,0:T(8,128)(2,1)} copy(bf16[16,3584]{1,0:T(8,128)(2,1)} %shard_map.127) | data formatting | bytes 229376

commit v7 on v6

--- a/solution.py
+++ b/solution.py
@@ -425,7 +425,7 @@
             piece_of = value[:, n * COL:(n + 1) * COL]
             yb[j] = yb[j] + piece_of if add else piece_of
 
-    pairs = [range(j, min(j + 2, n_col)) for j in range(0, n_col, 2)]
+    pairs = [range(max(j - 1, 0), j + 1) for j in range(0, n_col, 2)]
     landed(wa, wd_sem.at[0])
     for group in pairs[:2]:
         keep(group, down_half(core, group), False)

time: 42.3 us -> 42.7 us (level)
  Pallas kernels: 40.6 us -> 41.1 us
    pallas_call x1, Pallas kernels: 40.6 us -> 41.1 us  [device_fn(): pl.pallas_call(functools.partial(layer_kernel, n_dev, n_side), out_shape=...]
where the time goes in v7:
time: 42.7 us; the launch traced here: 42.6 us
  Pallas kernels  41.1 us (96%)
  local copies, waits for them, and re-layouts  1.55 us (4%)
    pallas_call x1, Pallas kernels, device_fn(): pl.pallas_call(functools.partial(layer_kernel, n_dev, n_side), out_shape=...  41.1 us
    unnamed x1, local copies, waits for them, and re-layouts  1.55 us

profile of v7, /device:TPU:97, one launch (start us, length us, event | category | flops | bytes accessed | tf_op | source)
XLA Modules:
  0.0 42.6 jit_solution(15449418281671114524)
XLA Ops:
  0.0 41.1 %shard_map.127 = bf16[16,3584]{1,0:T(8,128)(2,1)} custom-call(bf16[128,3584]{1,0:T(8,128)(2,1)} %x_hbm.1, s32[1,128]{1,0:T(1,128)} %bitcast.17, f32[1,128]{1,0:T(1,128)} %constant.3.freq_hbm, bf16[128,8,64,256]{3,2,1,0:T(8,128)(2,1)} %bitcast.9, bf16[128,8,64,256]{3,2,1,0:T(8,128)(2,1)} %bitcast.10, bf16[56,64,4096]{2,1,0:T(8,128)(2,1)} %bitcast.11, ...), custom_call_target="tpu_custom_call" | custom-call | tf_op jit(solution)/shard_map/pallas_call | solution.py:566
  41.1 1.6 %copy.15 = bf16[16,3584]{1,0:T(8,128)(2,1)} copy(bf16[16,3584]{1,0:T(8,128)(2,1)} %shard_map.127) | data formatting | bytes 229376
